TPU v7x, 256 devices: a whole 4x4x8 slice. The times are simulated.
256 devices in a mesh: tm: 64 (over z, x, core), asset: 4 (over y).
Axes of the slice: x: 4, y: 4, z: 8, core: 2. Of those that a mesh axis runs over, the one named last changes fastest.
Arguments:
- returns: float32 [1024, 2048], P('tm', 'asset'), may hold values from -6 to 6
- windows: int32 [64], P('tm'), may hold values from 20 to 250, as said below
- listed_from: int32 [2048], replicated, may hold values from 0 to 511
- listed_until: int32 [2048], replicated, may hold values from 512 to 1024
Outputs:
- correlation: float32 [64, 2048, 2048], P('tm', None, 'asset')
Inputs may be any that keep to these rules, and one draw needn't show every extreme that they name: `windows`: each window length is one of the four horizons max(256 * h // 256, 2) for h in 20, 60, 120, 250; the shortest and the longest both occur in every draw.
All inputs are finite; a program needn't handle non-finite values.
Results may differ from a plain program's by a relative error of at most 0.0003.
Values sent between devices are 32-bit elements; how exact they have to be, the bound alone decides.
A program may use at most 128 MiB of HBM per device.

v0:
```python
import jax
import jax.numpy as jnp
from jax import lax
from jax.sharding import PartitionSpec as P

SPAN = 256


highest = lax.Precision.HIGHEST


def sent_to_all(array, axis):
    devices = lax.axis_size(axis)
    return lax.all_to_all(
        jnp.broadcast_to(array[None], (devices, *array.shape)), axis, 0, 0, tiled=True
    )


def in_order(tiles, dim):
    tiles = jnp.moveaxis(tiles, 0, dim)
    lengths = tiles.shape
    return tiles.reshape(*lengths[:dim], lengths[dim] * lengths[dim + 1], *lengths[dim + 2 :])


def gather_directly(array, axis, dim):
    tiles = sent_to_all(array, axis)
    return in_order(tiles, dim)


def from_behind(array, axis, by):
    devices = lax.axis_size(axis)
    pairs = [(i, i + by) for i in range(devices) if 0 <= i + by < devices]
    return lax.ppermute(array, axis, pairs)


def cross_days(left_side, right_side):
    return lax.dot_general(
        left_side,
        right_side,
        (((0,), (0,)), ((), ())),
        precision=highest,
        preferred_element_type=jnp.float32,
    )


def six_sums(values_all, squared_all, listed_all, values_own, squared_own, listed_own):
    return (
        cross_days(values_all, values_own),
        cross_days(values_all, listed_own),
        cross_days(listed_all, values_own),
        cross_days(squared_all, listed_own),
        cross_days(listed_all, squared_own),
        cross_days(listed_all, listed_own),
    )


def correlate(cross_terms, sum_left, sum_right, square_left, square_right, pair_count):
    pairs = jnp.maximum(pair_count, 1.0)
    covariance = cross_terms - sum_left * sum_right / pairs
    var_left = jnp.maximum(square_left - sum_left * sum_left / pairs, 1.0)
    var_right = jnp.maximum(square_right - sum_right * sum_right / pairs, 1.0)
    return covariance / jnp.sqrt(var_left * var_right)


def on_device(returns, windows, listed_from, listed_until):
    group_rows, col_width = returns.shape
    span_rows = SPAN
    depth = span_rows // group_rows
    tm_pos = lax.axis_index("tm")
    col_pos = lax.axis_index("asset")
    group_all = gather_directly(returns, "asset", 1)
    pieces = [group_all]
    for offset in range(1, depth):
        pieces.insert(0, from_behind(group_all, "tm", offset))
    whole_rows = jnp.concatenate(pieces, axis=0)
    own_cols = lax.dynamic_slice_in_dim(whole_rows, col_pos * col_width, col_width, 1)
    end_day = (tm_pos + 1) * group_rows - 1
    window = windows[0]
    day_index = end_day - span_rows + 1 + jnp.arange(span_rows, dtype=jnp.int32)
    inside = (day_index > end_day - window) & (day_index >= 0)
    from_own = lax.dynamic_slice_in_dim(listed_from, col_pos * col_width, col_width, 0)
    until_own = lax.dynamic_slice_in_dim(listed_until, col_pos * col_width, col_width, 0)
    listed_all = (
        inside[:, None]
        & (listed_from[None, :] <= day_index[:, None])
        & (day_index[:, None] < listed_until[None, :])
    ).astype(jnp.float32)
    listed_own = (
        inside[:, None]
        & (from_own[None, :] <= day_index[:, None])
        & (day_index[:, None] < until_own[None, :])
    ).astype(jnp.float32)
    values_all = whole_rows * listed_all
    squared_all = values_all * values_all
    values_own = own_cols * listed_own
    squared_own = values_own * values_own
    totals = six_sums(values_all, squared_all, listed_all, values_own, squared_own, listed_own)
    cross_terms, sum_left, sum_right, square_left, square_right, pair_count = totals
    result = correlate(cross_terms, sum_left, sum_right, square_left, square_right, pair_count)
    return result[None]


def solution(mesh):
    placed = (P("tm", "asset"), P("tm"), P(), P())
    return jax.shard_map(
        on_device, mesh=mesh, in_specs=placed, out_specs=P("tm", None, "asset"), check_vma=False
    )
```

profile of v0, /device:TPU:129, one launch (start us, length us, event | category | flops | bytes accessed | tf_op | source)
XLA Modules:
  0.0 150.8 jit_solution(4885793254759893570)
XLA Ops:
  0.0 1.4 broadcast_in_dim.4
  1.4 4.2 %all-to-all-start = ((f32[4,16,512]{2,1,0:T(8,128)}), f32[4,16,512]{2,1,0:T(8,128)S(1)}, u32[]{:S(2)}, u32[]{:S(2)}) async-start(f32[4,16,512]{2,1,0:T(8,128)} %broadcast_in_dim.4), calls=%async_computation | async-start | bytes 262144 | tf_op jit(solution)/shard_map/all_to_all | solution.py:14
  6.3 0.8 dynamic_slice.9
  7.0 0.8 dynamic_slice.10
  7.8 2.6 %all-to-all-done = f32[4,16,512]{2,1,0:T(8,128)S(1)} async-done(((f32[4,16,512]{2,1,0:T(8,128)}), f32[4,16,512]{2,1,0:T(8,128)S(1)}, u32[]{:S(2)}, u32[]{:S(2)}) %all-to-all-start) | async-done | bytes 131104 | tf_op jit(solution)/shard_map/all_to_all | solution.py:14
  10.4 5.1 %collective-permute-start = (f32[16,2048]{1,0:T(8,128)S(1)}, f32[16,2048]{1,0:T(8,128)S(1)}, u32[]{:S(2)}, u32[]{:S(2)}) collective-permute-start(f32[16,2048]{1,0:T(8,128)S(1)} %bitcast.7), channel_id=1, source_target_pairs={{0,60},{4,64},{8,68},{12,72},{16,76},{20,80},{24,84},{28,88},{32,9... | collective-permute-start | bytes 393224 | tf_op jit(solution)/shard_map/ppermute | solution.py:33
  15.5 1.7 %fusion.26 = f32[2048,512]{1,0:T(8,128)S(1)} fusion(s32[512]{0:T(512)S(1)} %dynamic_slice.10, s32[512]{0:T(512)S(1)} %dynamic_slice.9, s32[256]{0:T(256)S(1)} %iota_add_fusion, pred[256]{0:T(512)(128)(4,1)S(1)} %compare_and_fusion.2, s32[2048]{0:T(1024)} %param.7, s32[2048]{0:T(1024)} %param.6), kind=kOutput, calls=%fused_computation.46 | convolution fusion | flops 539492352 | bytes 4216064 | tf_op jit(solution)/shard_map/dot_general | solution.py:37
  17.2 0.0 copy-start
  17.2 0.0 copy-start.1
  17.3 1.9 %collective-permute-start.14 = (f32[16,2048]{1,0:T(8,128)S(1)}, f32[16,2048]{1,0:T(8,128)S(1)}, u32[]{:S(2)}, u32[]{:S(2)}) collective-permute-start(f32[16,2048]{1,0:T(8,128)S(1)} %bitcast.8), channel_id=1, source_target_pairs={{0,4},{4,8},{8,12},{12,16},{16,20},{20,24},{24,28},{28,32},{32,36}... | collective-permute-start | bytes 393224 | tf_op jit(solution)/shard_map/ppermute | solution.py:33
  19.2 3.1 %collective-permute-start.13 = (f32[16,2048]{1,0:T(8,128)S(1)}, f32[16,2048]{1,0:T(8,128)S(1)}, u32[]{:S(2)}, u32[]{:S(2)}) collective-permute-start(f32[16,2048]{1,0:T(8,128)S(1)} %bitcast.9), channel_id=1, source_target_pairs={{0,8},{4,12},{8,16},{12,20},{16,24},{20,28},{24,32},{28,36},{32,40... | collective-permute-start | bytes 393224 | tf_op jit(solution)/shard_map/ppermute | solution.py:33
  22.3 5.0 %collective-permute-start.12 = (f32[16,2048]{1,0:T(8,128)S(1)}, f32[16,2048]{1,0:T(8,128)S(1)}, u32[]{:S(2)}, u32[]{:S(2)}) collective-permute-start(f32[16,2048]{1,0:T(8,128)S(1)} %bitcast.10), channel_id=1, source_target_pairs={{0,12},{4,16},{8,20},{12,24},{16,28},{20,32},{24,36},{28,40},{32,4... | collective-permute-start | bytes 393224 | tf_op jit(solution)/shard_map/ppermute | solution.py:33
  27.3 2.9 %collective-permute-start.11 = (f32[16,2048]{1,0:T(8,128)S(1)}, f32[16,2048]{1,0:T(8,128)S(1)}, u32[]{:S(2)}, u32[]{:S(2)}) collective-permute-start(f32[16,2048]{1,0:T(8,128)S(1)} %bitcast.11), channel_id=1, source_target_pairs={{0,16},{4,20},{8,24},{12,28},{16,32},{20,36},{24,40},{28,44},{32,4... | collective-permute-start | bytes 393224 | tf_op jit(solution)/shard_map/ppermute | solution.py:33
  30.2 0.0 collective-permute-done
  30.2 2.1 %collective-permute-start.1 = (f32[16,2048]{1,0:T(8,128)S(1)}, f32[16,2048]{1,0:T(8,128)S(1)}, u32[]{:S(2)}, u32[]{:S(2)}) collective-permute-start(f32[16,2048]{1,0:T(8,128)S(1)} %bitcast.12), channel_id=1, source_target_pairs={{0,56},{4,60},{8,64},{12,68},{16,72},{20,76},{24,80},{28,84},{32,8... | collective-permute-start | bytes 393224 | tf_op jit(solution)/shard_map/ppermute | solution.py:33
  32.4 8.7 %collective-permute-done.1 = f32[16,2048]{1,0:T(8,128)S(1)} collective-permute-done((f32[16,2048]{1,0:T(8,128)S(1)}, f32[16,2048]{1,0:T(8,128)S(1)}, u32[]{:S(2)}, u32[]{:S(2)}) %collective-permute-start.1) | collective-permute-done | bytes 131104 | tf_op jit(solution)/shard_map/ppermute | solution.py:33
  41.0 1.9 %collective-permute-start.2 = (f32[16,2048]{1,0:T(8,128)S(1)}, f32[16,2048]{1,0:T(8,128)S(1)}, u32[]{:S(2)}, u32[]{:S(2)}) collective-permute-start(f32[16,2048]{1,0:T(8,128)S(1)} %bitcast.13), channel_id=1, source_target_pairs={{0,52},{4,56},{8,60},{12,64},{16,68},{20,72},{24,76},{28,80},{32,8... | collective-permute-start | bytes 393224 | tf_op jit(solution)/shard_map/ppermute | solution.py:33
  43.0 12.1 %collective-permute-done.2 = f32[16,2048]{1,0:T(8,128)S(1)} collective-permute-done((f32[16,2048]{1,0:T(8,128)S(1)}, f32[16,2048]{1,0:T(8,128)S(1)}, u32[]{:S(2)}, u32[]{:S(2)}) %collective-permute-start.2) | collective-permute-done | bytes 131104 | tf_op jit(solution)/shard_map/ppermute | solution.py:33
  55.1 1.9 %collective-permute-start.3 = (f32[16,2048]{1,0:T(8,128)S(1)}, f32[16,2048]{1,0:T(8,128)S(1)}, u32[]{:S(2)}, u32[]{:S(2)}) collective-permute-start(f32[16,2048]{1,0:T(8,128)S(1)} %bitcast.14), channel_id=1, source_target_pairs={{0,48},{4,52},{8,56},{12,60},{16,64},{20,68},{24,72},{28,76},{32,8... | collective-permute-start | bytes 393224 | tf_op jit(solution)/shard_map/ppermute | solution.py:33
  57.0 9.1 %collective-permute-done.3 = f32[16,2048]{1,0:T(8,128)S(1)} collective-permute-done((f32[16,2048]{1,0:T(8,128)S(1)}, f32[16,2048]{1,0:T(8,128)S(1)}, u32[]{:S(2)}, u32[]{:S(2)}) %collective-permute-start.3) | collective-permute-done | bytes 131104 | tf_op jit(solution)/shard_map/ppermute | solution.py:33
  66.1 1.9 %collective-permute-start.4 = (f32[16,2048]{1,0:T(8,128)S(1)}, f32[16,2048]{1,0:T(8,128)S(1)}, u32[]{:S(2)}, u32[]{:S(2)}) collective-permute-start(f32[16,2048]{1,0:T(8,128)S(1)} %bitcast.15), channel_id=1, source_target_pairs={{0,44},{4,48},{8,52},{12,56},{16,60},{20,64},{24,68},{28,72},{32,7... | collective-permute-start | bytes 393224 | tf_op jit(solution)/shard_map/ppermute | solution.py:33
  68.0 10.4 %collective-permute-done.4 = f32[16,2048]{1,0:T(8,128)S(1)} collective-permute-done((f32[16,2048]{1,0:T(8,128)S(1)}, f32[16,2048]{1,0:T(8,128)S(1)}, u32[]{:S(2)}, u32[]{:S(2)}) %collective-permute-start.4) | collective-permute-done | bytes 131104 | tf_op jit(solution)/shard_map/ppermute | solution.py:33
  78.4 1.9 %collective-permute-start.5 = (f32[16,2048]{1,0:T(8,128)S(1)}, f32[16,2048]{1,0:T(8,128)S(1)}, u32[]{:S(2)}, u32[]{:S(2)}) collective-permute-start(f32[16,2048]{1,0:T(8,128)S(1)} %bitcast.16), channel_id=1, source_target_pairs={{0,40},{4,44},{8,48},{12,52},{16,56},{20,60},{24,64},{28,68},{32,7... | collective-permute-start | bytes 393224 | tf_op jit(solution)/shard_map/ppermute | solution.py:33
  80.4 8.3 %collective-permute-done.5 = f32[16,2048]{1,0:T(8,128)S(1)} collective-permute-done((f32[16,2048]{1,0:T(8,128)S(1)}, f32[16,2048]{1,0:T(8,128)S(1)}, u32[]{:S(2)}, u32[]{:S(2)}) %collective-permute-start.5) | collective-permute-done | bytes 131104 | tf_op jit(solution)/shard_map/ppermute | solution.py:33
  88.7 2.8 %collective-permute-start.6 = (f32[16,2048]{1,0:T(8,128)S(1)}, f32[16,2048]{1,0:T(8,128)S(1)}, u32[]{:S(2)}, u32[]{:S(2)}) collective-permute-start(f32[16,2048]{1,0:T(8,128)S(1)} %bitcast.17), channel_id=1, source_target_pairs={{0,36},{4,40},{8,44},{12,48},{16,52},{20,56},{24,60},{28,64},{32,6... | collective-permute-start | bytes 393224 | tf_op jit(solution)/shard_map/ppermute | solution.py:33
  91.5 4.9 %collective-permute-done.6 = f32[16,2048]{1,0:T(8,128)S(1)} collective-permute-done((f32[16,2048]{1,0:T(8,128)S(1)}, f32[16,2048]{1,0:T(8,128)S(1)}, u32[]{:S(2)}, u32[]{:S(2)}) %collective-permute-start.6) | collective-permute-done | bytes 131104 | tf_op jit(solution)/shard_map/ppermute | solution.py:33
  96.5 2.9 %collective-permute-start.7 = (f32[16,2048]{1,0:T(8,128)S(1)}, f32[16,2048]{1,0:T(8,128)S(1)}, u32[]{:S(2)}, u32[]{:S(2)}) collective-permute-start(f32[16,2048]{1,0:T(8,128)S(1)} %bitcast.18), channel_id=1, source_target_pairs={{0,32},{4,36},{8,40},{12,44},{16,48},{20,52},{24,56},{28,60},{32,6... | collective-permute-start | bytes 393224 | tf_op jit(solution)/shard_map/ppermute | solution.py:33
  99.4 4.0 %collective-permute-done.7 = f32[16,2048]{1,0:T(8,128)S(1)} collective-permute-done((f32[16,2048]{1,0:T(8,128)S(1)}, f32[16,2048]{1,0:T(8,128)S(1)}, u32[]{:S(2)}, u32[]{:S(2)}) %collective-permute-start.7) | collective-permute-done | bytes 131104 | tf_op jit(solution)/shard_map/ppermute | solution.py:33
  103.4 8.4 %collective-permute-start.8 = (f32[16,2048]{1,0:T(8,128)S(1)}, f32[16,2048]{1,0:T(8,128)S(1)}, u32[]{:S(2)}, u32[]{:S(2)}) collective-permute-start(f32[16,2048]{1,0:T(8,128)S(1)} %bitcast.19), channel_id=1, source_target_pairs={{0,28},{4,32},{8,36},{12,40},{16,44},{20,48},{24,52},{28,56},{32,6... | collective-permute-start | bytes 393224 | tf_op jit(solution)/shard_map/ppermute | solution.py:33
  111.8 1.9 %collective-permute-done.8 = f32[16,2048]{1,0:T(8,128)S(1)} collective-permute-done((f32[16,2048]{1,0:T(8,128)S(1)}, f32[16,2048]{1,0:T(8,128)S(1)}, u32[]{:S(2)}, u32[]{:S(2)}) %collective-permute-start.8) | collective-permute-done | bytes 131104 | tf_op jit(solution)/shard_map/ppermute | solution.py:33
  113.7 3.1 %collective-permute-start.9 = (f32[16,2048]{1,0:T(8,128)S(1)}, f32[16,2048]{1,0:T(8,128)S(1)}, u32[]{:S(2)}, u32[]{:S(2)}) collective-permute-start(f32[16,2048]{1,0:T(8,128)S(1)} %bitcast.20), channel_id=1, source_target_pairs={{0,24},{4,28},{8,32},{12,36},{16,40},{20,44},{24,48},{28,52},{32,5... | collective-permute-start | bytes 393224 | tf_op jit(solution)/shard_map/ppermute | solution.py:33
  116.9 4.7 %collective-permute-done.9 = f32[16,2048]{1,0:T(8,128)S(1)} collective-permute-done((f32[16,2048]{1,0:T(8,128)S(1)}, f32[16,2048]{1,0:T(8,128)S(1)}, u32[]{:S(2)}, u32[]{:S(2)}) %collective-permute-start.9) | collective-permute-done | bytes 131104 | tf_op jit(solution)/shard_map/ppermute | solution.py:33
  121.5 4.4 %collective-permute-start.10 = (f32[16,2048]{1,0:T(8,128)S(1)}, f32[16,2048]{1,0:T(8,128)S(1)}, u32[]{:S(2)}, u32[]{:S(2)}) collective-permute-start(f32[16,2048]{1,0:T(8,128)S(1)} %bitcast.21), channel_id=1, source_target_pairs={{0,20},{4,24},{8,28},{12,32},{16,36},{20,40},{24,44},{28,48},{32,5... | collective-permute-start | bytes 393224 | tf_op jit(solution)/shard_map/ppermute | solution.py:33
  125.9 6.6 %collective-permute-done.10 = f32[16,2048]{1,0:T(8,128)S(1)} collective-permute-done((f32[16,2048]{1,0:T(8,128)S(1)}, f32[16,2048]{1,0:T(8,128)S(1)}, u32[]{:S(2)}, u32[]{:S(2)}) %collective-permute-start.10) | collective-permute-done | bytes 131104 | tf_op jit(solution)/shard_map/ppermute | solution.py:33
  132.5 0.0 collective-permute-done.11
  132.6 0.0 collective-permute-done.12
  132.6 0.0 collective-permute-done.13
  132.6 0.0 collective-permute-done.14
  132.7 0.0 copy-done
  132.7 0.0 copy-done.1
  132.7 2.4 %fusion.3 = f32[2048,512]{1,0:T(8,128)S(1)} fusion(f32[256,2048]{1,0:T(8,128)S(1)} %constant_dynamic-update-slice_fusion, s32[512]{0:T(512)S(1)} %dynamic_slice.10, s32[512]{0:T(512)S(1)} %dynamic_slice.9, s32[256]{0:T(256)S(1)} %iota_add_fusion, pred[256]{0:T(512)(128)(4,1)S(1)} %compare_and_fusion.2, s32[2048]{0:T(1024)S(1)} %copy-done, s32[2048]{0:T(1024)S(1)} %copy-done.1), kind=kOutput, calls=%fused_computation.5 | convolution fusion | flops 3224371200 | bytes 6313216 | tf_op jit(solution)/shard_map/dot_general | solution.py:37
  135.1 2.4 %fusion = f32[2048,512]{1,0:T(8,128)S(1)} fusion(f32[256,2048]{1,0:T(8,128)S(1)} %constant_dynamic-update-slice_fusion, s32[512]{0:T(512)S(1)} %dynamic_slice.10, s32[512]{0:T(512)S(1)} %dynamic_slice.9, s32[256]{0:T(256)S(1)} %iota_add_fusion, pred[256]{0:T(512)(128)(4,1)S(1)} %compare_and_fusion.2, s32[2048]{0:T(1024)S(1)} %copy-done, s32[2048]{0:T(1024)S(1)} %copy-done.1), kind=kOutput, calls=%fused_computation.1 | convolution fusion | flops 3224895488 | bytes 6313216 | tf_op jit(solution)/shard_map/dot_general | solution.py:37
  137.6 2.2 %fusion.14 = f32[2048,512]{1,0:T(8,128)S(1)} fusion(f32[256,2048]{1,0:T(8,128)S(1)} %constant_dynamic-update-slice_fusion, s32[]{:T(128)S(6)} %select_n.2, s32[512]{0:T(512)S(1)} %dynamic_slice.10, s32[512]{0:T(512)S(1)} %dynamic_slice.9, s32[256]{0:T(256)S(1)} %iota_add_fusion, pred[256]{0:T(512)(128)(4,1)S(1)} %compare_and_fusion.2, ...), kind=kOutput, calls=%fused_computation.16 | convolution fusion | flops 3223977984 | bytes 4742148 | tf_op jit(solution)/shard_map/dot_general | solution.py:37
  139.8 4.3 %fusion.5 = f32[2048,512]{1,0:T(8,128)S(1)} fusion(f32[256,2048]{1,0:T(8,128)S(1)} %constant_dynamic-update-slice_fusion, s32[]{:T(128)S(6)} %select_n.2, s32[512]{0:T(512)S(1)} %dynamic_slice.10, s32[512]{0:T(512)S(1)} %dynamic_slice.9, s32[256]{0:T(256)S(1)} %iota_add_fusion, pred[256]{0:T(512)(128)(4,1)S(1)} %compare_and_fusion.2, s32[2048]{0:T(1024)S(1)} %copy-done, ...), kind=kOutput, calls=%fused_computation.7 | convolution fusion | flops 3224502272 | bytes 6839300 | tf_op jit(solution)/shard_map/dot_general | solution.py:37
  144.1 6.7 %multiply_bitcast_fusion = f32[1,2048,512]{2,1,0:T(8,128)} fusion(f32[2048,512]{1,0:T(8,128)S(1)} %fusion.14, f32[2048,512]{1,0:T(8,128)S(1)} %fusion, f32[2048,512]{1,0:T(8,128)S(1)} %fusion.3, f32[2048,512]{1,0:T(8,128)S(1)} %fusion.5, f32[2048,512]{1,0:T(8,128)S(1)} %fusion.26, f32[256,2048]{1,0:T(8,128)S(1)} %constant_dynamic-update-slice_fusion, ...), kind=kOutput, calls=%fused_computation | convolution fusion | flops 3238789120 | bytes 25713668 | tf_op jit(solution)/shard_map/dot_general | solution.py:37
  (19 shorter events, 0.2 us)
Async XLA Ops:
  1.4 9.0 %all-to-all-start = ((f32[4,16,512]{2,1,0:T(8,128)}), f32[4,16,512]{2,1,0:T(8,128)S(1)}, u32[]{:S(2)}, u32[]{:S(2)}) async-start(f32[4,16,512]{2,1,0:T(8,128)} %broadcast_in_dim.4), calls=%async_computation | async-start | bytes 262144 | tf_op jit(solution)/shard_map/all_to_all | solution.py:14
  10.4 19.8 %collective-permute-start = (f32[16,2048]{1,0:T(8,128)S(1)}, f32[16,2048]{1,0:T(8,128)S(1)}, u32[]{:S(2)}, u32[]{:S(2)}) collective-permute-start(f32[16,2048]{1,0:T(8,128)S(1)} %bitcast.7), channel_id=1, source_target_pairs={{0,60},{4,64},{8,68},{12,72},{16,76},{20,80},{24,84},{28,88},{32,9... | collective-permute-start | bytes 393224 | tf_op jit(solution)/shard_map/ppermute | solution.py:33
  17.2 115.5 %copy-start = (s32[2048]{0:T(1024)S(1)}, s32[2048]{0:T(1024)}, u32[]{:S(2)}) copy-start(s32[2048]{0:T(1024)} %param.7) | copy-start | bytes 24580
  17.2 115.5 %copy-start.1 = (s32[2048]{0:T(1024)S(1)}, s32[2048]{0:T(1024)}, u32[]{:S(2)}) copy-start(s32[2048]{0:T(1024)} %param.6) | copy-start | bytes 24580
  17.3 115.4 %collective-permute-start.14 = (f32[16,2048]{1,0:T(8,128)S(1)}, f32[16,2048]{1,0:T(8,128)S(1)}, u32[]{:S(2)}, u32[]{:S(2)}) collective-permute-start(f32[16,2048]{1,0:T(8,128)S(1)} %bitcast.8), channel_id=1, source_target_pairs={{0,4},{4,8},{8,12},{12,16},{16,20},{20,24},{24,28},{28,32},{32,36}... | collective-permute-start | bytes 393224 | tf_op jit(solution)/shard_map/ppermute | solution.py:33
  19.2 113.4 %collective-permute-start.13 = (f32[16,2048]{1,0:T(8,128)S(1)}, f32[16,2048]{1,0:T(8,128)S(1)}, u32[]{:S(2)}, u32[]{:S(2)}) collective-permute-start(f32[16,2048]{1,0:T(8,128)S(1)} %bitcast.9), channel_id=1, source_target_pairs={{0,8},{4,12},{8,16},{12,20},{16,24},{20,28},{24,32},{28,36},{32,40... | collective-permute-start | bytes 393224 | tf_op jit(solution)/shard_map/ppermute | solution.py:33
  22.3 110.2 %collective-permute-start.12 = (f32[16,2048]{1,0:T(8,128)S(1)}, f32[16,2048]{1,0:T(8,128)S(1)}, u32[]{:S(2)}, u32[]{:S(2)}) collective-permute-start(f32[16,2048]{1,0:T(8,128)S(1)} %bitcast.10), channel_id=1, source_target_pairs={{0,12},{4,16},{8,20},{12,24},{16,28},{20,32},{24,36},{28,40},{32,4... | collective-permute-start | bytes 393224 | tf_op jit(solution)/shard_map/ppermute | solution.py:33
  27.3 105.2 %collective-permute-start.11 = (f32[16,2048]{1,0:T(8,128)S(1)}, f32[16,2048]{1,0:T(8,128)S(1)}, u32[]{:S(2)}, u32[]{:S(2)}) collective-permute-start(f32[16,2048]{1,0:T(8,128)S(1)} %bitcast.11), channel_id=1, source_target_pairs={{0,16},{4,20},{8,24},{12,28},{16,32},{20,36},{24,40},{28,44},{32,4... | collective-permute-start | bytes 393224 | tf_op jit(solution)/shard_map/ppermute | solution.py:33
  30.2 10.8 %collective-permute-start.1 = (f32[16,2048]{1,0:T(8,128)S(1)}, f32[16,2048]{1,0:T(8,128)S(1)}, u32[]{:S(2)}, u32[]{:S(2)}) collective-permute-start(f32[16,2048]{1,0:T(8,128)S(1)} %bitcast.12), channel_id=1, source_target_pairs={{0,56},{4,60},{8,64},{12,68},{16,72},{20,76},{24,80},{28,84},{32,8... | collective-permute-start | bytes 393224 | tf_op jit(solution)/shard_map/ppermute | solution.py:33
  41.0 14.1 %collective-permute-start.2 = (f32[16,2048]{1,0:T(8,128)S(1)}, f32[16,2048]{1,0:T(8,128)S(1)}, u32[]{:S(2)}, u32[]{:S(2)}) collective-permute-start(f32[16,2048]{1,0:T(8,128)S(1)} %bitcast.13), channel_id=1, source_target_pairs={{0,52},{4,56},{8,60},{12,64},{16,68},{20,72},{24,76},{28,80},{32,8... | collective-permute-start | bytes 393224 | tf_op jit(solution)/shard_map/ppermute | solution.py:33
  55.1 11.0 %collective-permute-start.3 = (f32[16,2048]{1,0:T(8,128)S(1)}, f32[16,2048]{1,0:T(8,128)S(1)}, u32[]{:S(2)}, u32[]{:S(2)}) collective-permute-start(f32[16,2048]{1,0:T(8,128)S(1)} %bitcast.14), channel_id=1, source_target_pairs={{0,48},{4,52},{8,56},{12,60},{16,64},{20,68},{24,72},{28,76},{32,8... | collective-permute-start | bytes 393224 | tf_op jit(solution)/shard_map/ppermute | solution.py:33
  66.1 12.3 %collective-permute-start.4 = (f32[16,2048]{1,0:T(8,128)S(1)}, f32[16,2048]{1,0:T(8,128)S(1)}, u32[]{:S(2)}, u32[]{:S(2)}) collective-permute-start(f32[16,2048]{1,0:T(8,128)S(1)} %bitcast.15), channel_id=1, source_target_pairs={{0,44},{4,48},{8,52},{12,56},{16,60},{20,64},{24,68},{28,72},{32,7... | collective-permute-start | bytes 393224 | tf_op jit(solution)/shard_map/ppermute | solution.py:33
  78.4 10.3 %collective-permute-start.5 = (f32[16,2048]{1,0:T(8,128)S(1)}, f32[16,2048]{1,0:T(8,128)S(1)}, u32[]{:S(2)}, u32[]{:S(2)}) collective-permute-start(f32[16,2048]{1,0:T(8,128)S(1)} %bitcast.16), channel_id=1, source_target_pairs={{0,40},{4,44},{8,48},{12,52},{16,56},{20,60},{24,64},{28,68},{32,7... | collective-permute-start | bytes 393224 | tf_op jit(solution)/shard_map/ppermute | solution.py:33
  88.7 7.8 %collective-permute-start.6 = (f32[16,2048]{1,0:T(8,128)S(1)}, f32[16,2048]{1,0:T(8,128)S(1)}, u32[]{:S(2)}, u32[]{:S(2)}) collective-permute-start(f32[16,2048]{1,0:T(8,128)S(1)} %bitcast.17), channel_id=1, source_target_pairs={{0,36},{4,40},{8,44},{12,48},{16,52},{20,56},{24,60},{28,64},{32,6... | collective-permute-start | bytes 393224 | tf_op jit(solution)/shard_map/ppermute | solution.py:33
  96.5 6.9 %collective-permute-start.7 = (f32[16,2048]{1,0:T(8,128)S(1)}, f32[16,2048]{1,0:T(8,128)S(1)}, u32[]{:S(2)}, u32[]{:S(2)}) collective-permute-start(f32[16,2048]{1,0:T(8,128)S(1)} %bitcast.18), channel_id=1, source_target_pairs={{0,32},{4,36},{8,40},{12,44},{16,48},{20,52},{24,56},{28,60},{32,6... | collective-permute-start | bytes 393224 | tf_op jit(solution)/shard_map/ppermute | solution.py:33
  103.4 10.3 %collective-permute-start.8 = (f32[16,2048]{1,0:T(8,128)S(1)}, f32[16,2048]{1,0:T(8,128)S(1)}, u32[]{:S(2)}, u32[]{:S(2)}) collective-permute-start(f32[16,2048]{1,0:T(8,128)S(1)} %bitcast.19), channel_id=1, source_target_pairs={{0,28},{4,32},{8,36},{12,40},{16,44},{20,48},{24,52},{28,56},{32,6... | collective-permute-start | bytes 393224 | tf_op jit(solution)/shard_map/ppermute | solution.py:33
  113.7 7.8 %collective-permute-start.9 = (f32[16,2048]{1,0:T(8,128)S(1)}, f32[16,2048]{1,0:T(8,128)S(1)}, u32[]{:S(2)}, u32[]{:S(2)}) collective-permute-start(f32[16,2048]{1,0:T(8,128)S(1)} %bitcast.20), channel_id=1, source_target_pairs={{0,24},{4,28},{8,32},{12,36},{16,40},{20,44},{24,48},{28,52},{32,5... | collective-permute-start | bytes 393224 | tf_op jit(solution)/shard_map/ppermute | solution.py:33
  121.5 11.0 %collective-permute-start.10 = (f32[16,2048]{1,0:T(8,128)S(1)}, f32[16,2048]{1,0:T(8,128)S(1)}, u32[]{:S(2)}, u32[]{:S(2)}) collective-permute-start(f32[16,2048]{1,0:T(8,128)S(1)} %bitcast.21), channel_id=1, source_target_pairs={{0,20},{4,24},{8,28},{12,32},{16,36},{20,40},{24,44},{28,48},{32,5... | collective-permute-start | bytes 393224 | tf_op jit(solution)/shard_map/ppermute | solution.py:33
where the time goes:
time: 152 us; the launch traced here: 151 us
  waiting for transfers between devices  73.3 us (48%)
  starting transfers between devices  53.6 us (35%)
  matrix products  19.7 us (13%)
  local copies, waits for them, and re-layouts  3.15 us (2%)
    ppermute x15, waiting for transfers between devices, from_behind(): return lax.ppermute(array, axis, pairs)  70.6 us
    ppermute x15, starting transfers between devices, from_behind(): return lax.ppermute(array, axis, pairs)  49.4 us
    dot_general x6, matrix products, cross_days(): lax.dot_general(left_side, right_side, (((0,), (0,)), ((), ())), precisio...  19.7 us
    all_to_all x1, starting transfers between devices, sent_to_all(): lax.all_to_all(jnp.broadcast_to(array[None], (devices, *array.shape)), ax...  4.18 us
  transfers between devices with their start and end apart: 16, of which 11 were waited for; matrix products, arithmetic and copies ran while one was open for 2% of the time, Pallas kernels for 0%

commit v1 on v0

v1 whole, which is shorter than its diff:
```python
import functools

import jax
import jax.numpy as jnp
from jax import lax
from jax.experimental import pallas as pl
from jax.experimental.pallas import tpu as pltpu
from jax.sharding import PartitionSpec as P

MESH = pl.DeviceIdType.MESH
F32, BF16 = jnp.float32, jnp.bfloat16
NZ, NX, NY = 8, 4, 4
GROUP, HALF, SPAN = 16, 8, 256
COLS, ASSETS = 512, 2048

Z_SEM = 0
YS_SEM = Z_SEM + 4
YSR_SEM = YS_SEM + 12
XA_SEM = YSR_SEM + 6
XAR_SEM = XA_SEM + 4
XB_SEM = XAR_SEM + 2
XBR_SEM = XB_SEM + 16
YA_SEM = XBR_SEM + 8
YAR_SEM = YA_SEM + 6
D_SEM = YAR_SEM + 6
N_SEM = D_SEM + 8


def gather_kernel(returns_ref, all_ref, own, ss, rs, local_sem):
    tm, y = lax.axis_index("tm"), lax.axis_index("asset")
    z, x, c = tm // 8, (tm // 2) % 4, tm % 2

    def dev(dz=0, dx=0, dy=0, dc=0):
        return (
            ((z + dz) % NZ) * 8 + ((x + dx) % NX) * 2 + (c + dc) % 2,
            (y + dy) % NY,
        )

    partner = dev(dc=1)

    def copy(src, dst, i, to):
        return pltpu.make_async_remote_copy(
            src_ref=src, dst_ref=dst, send_sem=ss.at[i], recv_sem=rs.at[i], device_id=to, device_id_type=MESH
        )

    def received(dst, i):
        copy(dst, dst, i, partner).wait_recv()

    def send(src, dst, i, to):
        copy(src, dst, i, to).start()

    loads = [
        pltpu.make_async_copy(returns_ref.at[pl.ds(h * HALF, HALF)], own.at[h, y, 0], local_sem.at[h]) for h in (0, 1)
    ]
    for load in loads:
        load.start()
    barrier = pltpu.get_barrier_semaphore()
    peers = [dev(dz=1), dev(dz=-1), dev(dz=2), dev(dz=-2), dev(dx=1), dev(dx=-1), dev(dy=1), dev(dy=-1), partner]
    for peer in peers:
        pl.semaphore_signal(barrier, inc=1, device_id=peer, device_id_type=MESH)
    pl.semaphore_wait(barrier, len(peers))
    for load in loads:
        load.wait()

    step = (1, -1)

    def ring_x(dx):
        return (x + dx) % NX

    def z_send(h, k):
        send(own.at[h, y, 0], own.at[h, y, k], Z_SEM + h * 2 + k - 1, dev(dz=k))

    def z_wait(k):
        for h in (0, 1):
            received(own.at[h, y, k], Z_SEM + h * 2 + k - 1)

    def ys_send(k):
        for h in (0, 1):
            for d in (0, 1):
                send(own.at[h, y, k], own.at[h, y, k], YS_SEM + h * 6 + k * 2 + d, dev(dy=step[d]))

    def ys_wait(k):
        for h in (0, 1):
            for d in (0, 1):
                origin = (y - step[d]) % NY
                received(own.at[h, origin, k], YS_SEM + h * 6 + k * 2 + d)
                if (h + k) % 2 == d:
                    send(own.at[h, origin, k], own.at[h, origin, k], YSR_SEM + h * 3 + k, dev(dy=step[d]))

    def ysr_wait(k):
        for h in (0, 1):
            received(own.at[h, (y + 2) % NY, k], YSR_SEM + h * 3 + k)

    def x_send(h, j, k):
        base = XA_SEM if h == 0 else XB_SEM + j * 4
        at = (y + j) % NY
        for d in (0, 1):
            to = ring_x(step[d])
            up = to > x

            def go(slot):
                send(
                    own.at[h, at, k],
                    all_ref.at[at, c, h, x, slot],
                    base + d * 2 + slot,
                    dev(dx=step[d]),
                )

            if k == 1:
                go(up.astype(jnp.int32))
            elif k == 0:
                pl.when(up)(lambda: go(0))
            else:
                pl.when(jnp.logical_not(up))(lambda: go(1))

    def x_wait(h, j):
        base, relay = (XA_SEM, XAR_SEM) if h == 0 else (XB_SEM + j * 4, XBR_SEM + j * 2)
        at = (y + j) % NY
        first = (jnp.where(x == 3, 1, 0), jnp.where(x == 0, 0, 1))
        for d in (0, 1):
            origin = ring_x(-step[d])
            received(all_ref.at[at, c, h, origin, first[d]], base + d * 2 + first[d])
            send(all_ref.at[at, c, h, origin, first[d]], all_ref.at[at, c, h, origin, d], relay + d, dev(dx=step[d]))
        for d in (0, 1):
            origin = ring_x(-step[d])
            received(all_ref.at[at, c, h, origin, 1 - first[d]], base + d * 2 + 1 - first[d])

    def xr_wait(h, j):
        relay = XAR_SEM if h == 0 else XBR_SEM + j * 2
        at = (y + j) % NY
        for d in (0, 1):
            received(all_ref.at[at, c, h, ring_x(2), d], relay + d)

    def ya_send(dist):
        at = ring_x(-dist)
        for d in (0, 1):
            view = all_ref.at[y, c, 0, at]
            send(view, view, YA_SEM + (dist - 1) * 2 + d, dev(dy=step[d]))

    def ya_wait(dist):
        at = ring_x(-dist)
        for d in (0, 1):
            origin = (y - step[d]) % NY
            received(all_ref.at[origin, c, 0, at], YA_SEM + (dist - 1) * 2 + d)
            view = all_ref.at[origin, c, 0, at, d]
            send(view, view, YAR_SEM + (dist - 1) * 2 + d, dev(dy=step[d]))

    def yar_wait(dist):
        at = ring_x(-dist)
        for d in (0, 1):
            received(all_ref.at[(y + 2) % NY, c, 0, at, d], YAR_SEM + (dist - 1) * 2 + d)

    def to_partner(h, dist):
        at = ring_x(-dist)
        if dist == 0:
            send(own.at[h, :, pl.ds(c, 2)], all_ref.at[:, c, h, x], D_SEM + h * 4, partner)
        else:
            send(all_ref.at[:, c, h, at], all_ref.at[:, c, h, at], D_SEM + h * 4 + dist, partner)

    def from_partner(h, dist):
        received(all_ref.at[:, 1 - c, h, ring_x(-dist)], D_SEM + h * 4 + dist)

    for k in (1, 2):
        for h in (0, 1):
            z_send(h, k)
    ys_send(0)
    x_send(0, 0, 0)
    x_send(1, 0, 0)
    ys_wait(0)
    x_send(1, 1, 0)
    x_send(1, 3, 0)
    z_wait(1)
    x_send(0, 0, 1)
    ys_send(1)
    x_send(1, 0, 1)
    z_wait(2)
    x_send(0, 0, 2)
    ys_send(2)
    x_send(1, 0, 2)
    ysr_wait(0)
    x_send(1, 2, 0)
    ys_wait(1)
    x_send(1, 1, 1)
    x_send(1, 3, 1)
    x_wait(0, 0)
    ya_send(1)
    ya_send(3)
    ys_wait(2)
    x_send(1, 1, 2)
    x_send(1, 3, 2)
    x_wait(1, 0)
    ysr_wait(1)
    x_send(1, 2, 1)
    xr_wait(0, 0)
    ya_send(2)
    ysr_wait(2)
    x_send(1, 2, 2)
    to_partner(0, 0)
    to_partner(1, 0)
    all_ref[:, pl.ds(c, 1), :, pl.ds(x, 1)] = jnp.swapaxes(own[:, :, 0:2], 0, 1)[:, None, :, None]
    x_wait(1, 1)
    x_wait(1, 3)
    ya_wait(1)
    ya_wait(3)
    x_wait(1, 2)
    to_partner(1, 1)
    to_partner(1, 3)
    ya_wait(2)
    for j in range(4):
        xr_wait(1, j)
    to_partner(1, 2)
    yar_wait(1)
    to_partner(0, 1)
    yar_wait(3)
    to_partner(0, 3)
    yar_wait(2)
    to_partner(0, 2)
    for h, dist in ((0, 0), (1, 0), (1, 1), (1, 3), (1, 2), (0, 1), (0, 3), (0, 2)):
        from_partner(h, dist)

    block, two = own.at[0, 0, 0], own.at[0, 0, pl.ds(0, 2)]
    many = all_ref.at[:, 0, 0, 0]
    for i in range(N_SEM):
        view = many if i >= D_SEM else two if YA_SEM <= i < YAR_SEM else block
        copy(view, view, i, partner).wait_send()


def gathered(returns):
    return pl.pallas_call(
        gather_kernel,
        out_shape=jax.ShapeDtypeStruct((NY, 2, 2, NX, 2, HALF, COLS), F32),
        in_specs=[pl.BlockSpec(memory_space=pl.ANY)],
        out_specs=pl.BlockSpec(memory_space=pltpu.VMEM),
        scratch_shapes=[
            pltpu.VMEM((2, NY, 3, HALF, COLS), F32),
            pltpu.SemaphoreType.DMA((N_SEM,)),
            pltpu.SemaphoreType.DMA((N_SEM,)),
            pltpu.SemaphoreType.DMA((2,)),
        ],
        compiler_params=pltpu.CompilerParams(collective_id=0, has_side_effects=True),
    )(returns)


def day_of(row, tm):
    core, half, at, slot, day = row // 128, (row // 64) % 2, (row // 16) % 4, (row // 8) % 2, row % 8
    place = at * 2 + core
    back = slot + (place > tm % 8).astype(jnp.int32)
    return ((tm // 8 - back) * 8 + place) * GROUP + half * HALF + day


def split(value):
    high = value.astype(BF16)
    return high, (value - high.astype(F32)).astype(BF16)


def dot(left, right):
    return jnp.dot(left, right, preferred_element_type=F32)


ROWS = 256
TILE = 256


def correlate_kernel(windows_ref, from_ref, until_ref, all_ref, out_ref, high_r, low_r, live_r, sq_high_r, sq_low_r):
    tm, y = lax.axis_index("tm"), lax.axis_index("asset")
    g = pl.program_id(0)
    end = (tm + 1) * GROUP
    begin = jnp.maximum(end - windows_ref[0], 0)

    def spans(at, width):
        first = jnp.maximum(from_ref[:, pl.ds(at, width)], begin).astype(F32)
        last = jnp.minimum(until_ref[:, pl.ds(at, width)], end).astype(F32)
        return first, last

    @pl.when(g == 0)
    def _():
        first, last = spans(pl.multiple_of(y * COLS, COLS), COLS)
        day = day_of(lax.broadcasted_iota(jnp.int32, (SPAN, COLS), 0), tm).astype(F32)
        live = (day >= first) & (day < last)
        value = jnp.where(live, all_ref[y], 0.0)
        high_r[...], low_r[...] = split(value)
        live_r[...] = live.astype(F32).astype(BF16)
        sq_high_r[...], sq_low_r[...] = split(value * value)

    first, last = spans(pl.multiple_of(g * ROWS, ROWS), ROWS)
    first_t = jnp.broadcast_to(first, (128, ROWS)).T
    last_t = jnp.broadcast_to(last, (128, ROWS)).T
    raw = all_ref[g // 2, :, pl.ds(pl.multiple_of((g % 2) * ROWS, ROWS), ROWS)]
    day = day_of(lax.broadcasted_iota(jnp.int32, (ROWS, SPAN), 1), tm).astype(F32)
    wide = jnp.concatenate([first_t, first_t], axis=1), jnp.concatenate([last_t, last_t], axis=1)
    live = (day >= wide[0]) & (day < wide[1])
    value = jnp.where(live, raw.T, 0.0)
    high, low = split(value)
    sq_high, sq_low = split(value * value)
    live = live.astype(F32).astype(BF16)
    own_first, own_last = spans(pl.multiple_of(y * COLS, COLS), COLS)
    for n in range(0, COLS, TILE):
        at = slice(n, n + TILE)
        high_o, low_o, live_o = high_r[:, at], low_r[:, at], live_r[:, at]
        cross = dot(high, high_o) + dot(low, high_o) + dot(high, low_o)
        sum_l = dot(high, live_o) + dot(low, live_o)
        square_l = dot(sq_high, live_o) + dot(sq_low, live_o)
        sum_r = dot(live, high_o) + dot(live, low_o)
        square_r = dot(live, sq_high_r[:, at]) + dot(live, sq_low_r[:, at])
        pairs = jnp.minimum(wide[1], own_last[:, at]) - jnp.maximum(wide[0], own_first[:, at])
        pairs = jnp.maximum(pairs, 1.0)
        covariance = pairs * cross - sum_l * sum_r
        var_l = jnp.maximum(pairs * square_l - sum_l * sum_l, pairs)
        var_r = jnp.maximum(pairs * square_r - sum_r * sum_r, pairs)
        out_ref[:, at] = covariance * lax.rsqrt(var_l * var_r)


def correlated(windows, listed_from, listed_until, whole):
    full = lambda *shape: pl.BlockSpec(shape, lambda g: (0,) * len(shape))
    return pl.pallas_call(
        correlate_kernel,
        grid=(ASSETS // ROWS,),
        out_shape=jax.ShapeDtypeStruct((ASSETS, COLS), F32),
        in_specs=[
            pl.BlockSpec(memory_space=pltpu.SMEM),
            full(1, ASSETS),
            full(1, ASSETS),
            full(NY, SPAN, COLS),
        ],
        out_specs=pl.BlockSpec((ROWS, COLS), lambda g: (g, 0)),
        scratch_shapes=[pltpu.VMEM((SPAN, COLS), BF16)] * 5,
        compiler_params=pltpu.CompilerParams(dimension_semantics=("arbitrary",)),
    )(windows, listed_from[None], listed_until[None], whole)


def on_device(returns, windows, listed_from, listed_until):
    whole = gathered(returns).reshape(NY, SPAN, COLS)
    return correlated(windows, listed_from, listed_until, whole)[None]


def solution(mesh):
    placed = (P("tm", "asset"), P("tm"), P(), P())
    return jax.shard_map(
        on_device, mesh=mesh, in_specs=placed, out_specs=P("tm", None, "asset"), check_vma=False
    )
```

time: 152 us -> 45.2 us (0.30)
  the two profiles are of different devices: /device:TPU:129 before, /device:TPU:1 now
where the time goes in v1:
time: 45.2 us; the launch traced here: 45.1 us
  Pallas kernels  44.4 us (98%)
  between operations  0.66 us (1%)
    pallas_call x1, Pallas kernels, gathered(): pl.pallas_call(gather_kernel, out_shape=jax.ShapeDtypeStruct((NY, 2, 2, N...  32.3 us
    pallas_call x1, Pallas kernels, correlated(): pl.pallas_call(correlate_kernel, grid=(ASSETS // ROWS,), out_shape=jax.Sh...  12.1 us

profile of v1, /device:TPU:1, one launch (start us, length us, event | category | flops | bytes accessed | tf_op | source)
XLA Modules:
  0.0 45.1 jit_solution(11844048501758716161)
XLA Ops:
  0.7 32.3 %shard_map.46 = f32[4,2,2,4,2,8,512]{6,5,4,3,2,1,0:T(8,128)} custom-call(f32[16,512]{1,0:T(8,128)} %returns_ref.1), custom_call_target="tpu_custom_call" | custom-call | tf_op jit(solution)/shard_map/pallas_call | solution.py:229
  33.0 12.1 %shard_map.47 = f32[2048,512]{1,0:T(8,128)} custom-call(s32[1]{0:T(128)S(6)} %copy.5.windows_ref, s32[1,2048]{1,0:T(1,128)} %bitcast.5, s32[1,2048]{1,0:T(1,128)} %bitcast.6, f32[4,256,512]{2,1,0:T(8,128)} %bitcast.4), custom_call_target="tpu_custom_call" | custom-call | tf_op jit(solution)/shard_map/pallas_call | solution.py:315

commit v2 on v1

v2 whole, which is shorter than its diff:
```python
import functools

import jax
import jax.numpy as jnp
from jax import lax
from jax.experimental import pallas as pl
from jax.experimental.pallas import tpu as pltpu
from jax.sharding import PartitionSpec as P

MESH = pl.DeviceIdType.MESH
F32, BF16 = jnp.float32, jnp.bfloat16
NZ, NX, NY = 8, 4, 4
GROUP, HALF, SPAN = 16, 8, 256
COLS, ASSETS = 512, 2048

Z_SEM = 0
YS_SEM = Z_SEM + 4
YSR_SEM = YS_SEM + 12
XA_SEM = YSR_SEM + 6
XAR_SEM = XA_SEM + 4
XB_SEM = XAR_SEM + 2
XBR_SEM = XB_SEM + 16
YA_SEM = XBR_SEM + 8
YAR_SEM = YA_SEM + 6
D_SEM = YAR_SEM + 6
E_SEM = D_SEM + 4
N_SEM = E_SEM + 4
DIRECT = frozenset({"ys", "ya", "xA", "xB"})


def gather_kernel(returns_ref, all_ref, back2, extra, ss, rs, local_sem):
    tm, y = lax.axis_index("tm"), lax.axis_index("asset")
    z, x, c = tm // 8, (tm // 2) % 4, tm % 2

    def dev(dz=0, dx=0, dy=0, dc=0):
        return (
            ((z + dz) % NZ) * 8 + ((x + dx) % NX) * 2 + (c + dc) % 2,
            (y + dy) % NY,
        )

    partner = dev(dc=1)

    def copy(src, dst, i, to):
        return pltpu.make_async_remote_copy(
            src_ref=src, dst_ref=dst, send_sem=ss.at[i], recv_sem=rs.at[i], device_id=to, device_id_type=MESH
        )

    def received(dst, i):
        copy(dst, dst, i, partner).wait_recv()

    def send(src, dst, i, to):
        copy(src, dst, i, to).start()

    def origin_block(h, at, k):
        return all_ref.at[at, c, h, x, k] if k < 2 else back2.at[h, at]

    loads = [
        pltpu.make_async_copy(returns_ref.at[pl.ds(h * HALF, HALF)], origin_block(h, y, 0), local_sem.at[h])
        for h in (0, 1)
    ]
    for load in loads:
        load.start()
    barrier = pltpu.get_barrier_semaphore()

    def greet(peer):
        pl.semaphore_signal(barrier, inc=1, device_id=peer, device_id_type=MESH)

    flat = [dev(dx=1), dev(dx=-1), dev(dy=1), dev(dy=-1), partner]
    if DIRECT & {"xA", "xB"}:
        flat.append(dev(dx=2))
    if DIRECT & {"ys", "ya"}:
        flat.append(dev(dy=2))
    for k in (1, 2):
        pl.when(z >= k)(functools.partial(greet, dev(dz=-k)))
    for peer in flat:
        greet(peer)
    pl.semaphore_wait(barrier, len(flat) + jnp.minimum(NZ - 1 - z, 2))
    for load in loads:
        load.wait()

    step = (1, -1)

    def ring_x(dx):
        return (x + dx) % NX

    def z_send(h, k):
        @pl.when(z + k < NZ)
        def _():
            send(origin_block(h, y, 0), origin_block(h, y, k), Z_SEM + h * 2 + k - 1, dev(dz=k))

    def z_wait(k):
        @pl.when(z >= k)
        def _():
            for h in (0, 1):
                received(origin_block(h, y, k), Z_SEM + h * 2 + k - 1)

    def ys_send(k):
        for h in (0, 1):
            block = origin_block(h, y, k)
            for d in (0, 1):
                send(block, block, YS_SEM + h * 6 + k * 2 + d, dev(dy=step[d]))
            if "ys" in DIRECT:
                send(block, block, YSR_SEM + h * 3 + k, dev(dy=2))

    def ys_wait(k):
        for h in (0, 1):
            for d in (0, 1):
                block = origin_block(h, (y - step[d]) % NY, k)
                received(block, YS_SEM + h * 6 + k * 2 + d)
                if (h + k) % 2 == d and "ys" not in DIRECT:
                    send(block, block, YSR_SEM + h * 3 + k, dev(dy=step[d]))

    def ysr_wait(k):
        for h in (0, 1):
            received(origin_block(h, (y + 2) % NY, k), YSR_SEM + h * 3 + k)

    def x_send(h, j, k):
        direct = "xAxB"[h * 2 : h * 2 + 2] in DIRECT
        base, relay = (XA_SEM, XAR_SEM) if h == 0 else (XB_SEM + j * 4, XBR_SEM + j * 2)
        at = (y + j) % NY
        for d in (0, 1, 2)[: 2 + direct]:
            dx = (1, -1, 2)[d]
            up = ring_x(dx) > x

            def go(slot, d=d, dx=dx):
                sem = relay + slot if d == 2 else base + d * 2 + slot
                send(origin_block(h, at, k), all_ref.at[at, c, h, x, slot], sem, dev(dx=dx))

            if k == 1:
                go(up.astype(jnp.int32))
            elif k == 0:
                pl.when(up)(functools.partial(go, 0))
            else:
                pl.when(jnp.logical_not(up))(functools.partial(go, 1))

    def x_wait(h, j):
        direct = "xAxB"[h * 2 : h * 2 + 2] in DIRECT
        base, relay = (XA_SEM, XAR_SEM) if h == 0 else (XB_SEM + j * 4, XBR_SEM + j * 2)
        at = (y + j) % NY
        first = (0, 1) if direct else (jnp.where(x == 3, 1, 0), jnp.where(x == 0, 0, 1))
        for d in (0, 1):
            block = all_ref.at[at, c, h, ring_x(-step[d]), first[d]]
            received(block, base + d * 2 + first[d])
            if not direct:
                send(block, all_ref.at[at, c, h, ring_x(-step[d]), d], relay + d, dev(dx=step[d]))
        for d in (0, 1):
            received(all_ref.at[at, c, h, ring_x(-step[d]), 1 - first[d]], base + d * 2 + 1 - first[d])

    def xr_wait(h, j):
        relay = XAR_SEM if h == 0 else XBR_SEM + j * 2
        for d in (0, 1):
            received(all_ref.at[(y + j) % NY, c, h, ring_x(2), d], relay + d)

    def ya_send(dist):
        view = all_ref.at[y, c, 0, ring_x(-dist)]
        for d in (0, 1):
            send(view, view, YA_SEM + (dist - 1) * 2 + d, dev(dy=step[d]))
        if "ya" in DIRECT:
            for d in (0, 1):
                send(view.at[d], view.at[d], YAR_SEM + (dist - 1) * 2 + d, dev(dy=2))

    def ya_wait(dist):
        for d in (0, 1):
            view = all_ref.at[(y - step[d]) % NY, c, 0, ring_x(-dist)]
            received(view, YA_SEM + (dist - 1) * 2 + d)
            if "ya" not in DIRECT:
                send(view.at[d], view.at[d], YAR_SEM + (dist - 1) * 2 + d, dev(dy=step[d]))

    def yar_wait(dist):
        for d in (0, 1):
            received(all_ref.at[(y + 2) % NY, c, 0, ring_x(-dist), d], YAR_SEM + (dist - 1) * 2 + d)

    def to_partner(j):
        at = (y + j) % NY
        send(all_ref.at[at, c], all_ref.at[at, c], D_SEM + j, partner)

        @pl.when(c == 1)
        def _():
            send(back2.at[:, at], extra.at[:, at], E_SEM + j, partner)

    def from_partner(j):
        at = (y + j) % NY
        received(all_ref.at[at, 1 - c], D_SEM + j)

        @pl.when(c == 0)
        def _():
            received(extra.at[:, at], E_SEM + j)
            all_ref[at, 1, :, x, 0] = extra[:, at]

    for k in (1, 2):
        for h in (0, 1):
            z_send(h, k)
    ys_send(0)
    x_send(0, 0, 0)
    x_send(1, 0, 0)
    ys_wait(0)
    x_send(1, 1, 0)
    x_send(1, 3, 0)
    z_wait(1)
    x_send(0, 0, 1)
    ys_send(1)
    x_send(1, 0, 1)
    ysr_wait(0)
    x_send(1, 2, 0)
    z_wait(2)
    x_send(0, 0, 2)
    ys_send(2)
    x_send(1, 0, 2)
    ys_wait(1)
    x_send(1, 1, 1)
    x_send(1, 3, 1)
    x_wait(0, 0)
    ya_send(1)
    ya_send(3)
    x_wait(1, 0)
    ysr_wait(1)
    x_send(1, 2, 1)
    ys_wait(2)
    x_send(1, 1, 2)
    x_send(1, 3, 2)
    xr_wait(0, 0)
    ya_send(2)
    ysr_wait(2)
    x_send(1, 2, 2)
    xr_wait(1, 0)
    to_partner(0)
    ya_wait(1)
    ya_wait(3)
    x_wait(1, 1)
    x_wait(1, 3)
    x_wait(1, 2)
    ya_wait(2)
    xr_wait(1, 1)
    to_partner(1)
    xr_wait(1, 3)
    to_partner(3)
    xr_wait(1, 2)
    for dist in (1, 3, 2):
        yar_wait(dist)
    to_partner(2)
    for j in (0, 1, 3, 2):
        from_partner(j)

    block, two, many = back2.at[0, 0], all_ref.at[0, 0, 0, 0], all_ref.at[0, 0]
    for i in range(E_SEM):
        view = many if i >= D_SEM else two if YA_SEM <= i < YAR_SEM else block
        done = copy(view, view, i, partner).wait_send
        if i < YS_SEM:
            pl.when(z + 1 + i % 2 < NZ)(done)
        else:
            done()

    @pl.when(c == 1)
    def _():
        for j in range(4):
            copy(back2.at[:, 0], extra.at[:, 0], E_SEM + j, partner).wait_send()


def gathered(returns):
    return pl.pallas_call(
        gather_kernel,
        out_shape=jax.ShapeDtypeStruct((NY, 2, 2, NX, 2, HALF, COLS), F32),
        in_specs=[pl.BlockSpec(memory_space=pltpu.HBM)],
        out_specs=pl.BlockSpec(memory_space=pltpu.VMEM),
        scratch_shapes=[
            pltpu.VMEM((2, NY, HALF, COLS), F32),
            pltpu.VMEM((2, NY, HALF, COLS), F32),
            pltpu.SemaphoreType.DMA((N_SEM,)),
            pltpu.SemaphoreType.DMA((N_SEM,)),
            pltpu.SemaphoreType.DMA((2,)),
        ],
        compiler_params=pltpu.CompilerParams(collective_id=0, has_side_effects=True, vmem_limit_bytes=8 << 20),
    )(returns)


def day_of(row, tm):
    core, half, at, slot, day = row // 128, (row // 64) % 2, (row // 16) % 4, (row // 8) % 2, row % 8
    place = at * 2 + core
    later = (at > (tm // 2) % 4).astype(jnp.int32)
    back = jnp.where((place == tm % 8 + 1) & (core == 1), 2 - slot, slot + later)
    return ((tm // 8 - back) * 8 + place) * GROUP + half * HALF + day


def split(value):
    high = value.astype(BF16)
    return high, (value - high.astype(F32)).astype(BF16)


def dot(left, right):
    return jnp.dot(left, right, preferred_element_type=F32)


ROWS = 256
TILE = 256


def correlate_kernel(windows_ref, from_ref, until_ref, all_ref, out_ref, high_r, low_r, live_r, sq_high_r, sq_low_r):
    tm, y = lax.axis_index("tm"), lax.axis_index("asset")
    g = pl.program_id(0)
    end = (tm + 1) * GROUP
    begin = jnp.maximum(end - windows_ref[0], 0)

    def spans(at, width):
        first = jnp.maximum(from_ref[:, pl.ds(at, width)], begin).astype(F32)
        last = jnp.minimum(until_ref[:, pl.ds(at, width)], end).astype(F32)
        return first, last

    @pl.when(g == 0)
    def _():
        first, last = spans(pl.multiple_of(y * COLS, COLS), COLS)
        day = day_of(lax.broadcasted_iota(jnp.int32, (SPAN, COLS), 0), tm).astype(F32)
        live = (day >= first) & (day < last)
        value = jnp.where(live, all_ref[y], 0.0)
        high_r[...], low_r[...] = split(value)
        live_r[...] = live.astype(F32).astype(BF16)
        sq_high_r[...], sq_low_r[...] = split(value * value)

    first, last = spans(pl.multiple_of(g * ROWS, ROWS), ROWS)
    first_t = jnp.broadcast_to(first, (128, ROWS)).T
    last_t = jnp.broadcast_to(last, (128, ROWS)).T
    raw = all_ref[g // 2, :, pl.ds(pl.multiple_of((g % 2) * ROWS, ROWS), ROWS)]
    day = day_of(lax.broadcasted_iota(jnp.int32, (ROWS, SPAN), 1), tm).astype(F32)
    wide = jnp.concatenate([first_t, first_t], axis=1), jnp.concatenate([last_t, last_t], axis=1)
    live = (day >= wide[0]) & (day < wide[1])
    value = jnp.where(live, raw.T, 0.0)
    high, low = split(value)
    sq_high, sq_low = split(value * value)
    live = live.astype(F32).astype(BF16)
    own_first, own_last = spans(pl.multiple_of(y * COLS, COLS), COLS)
    for n in range(0, COLS, TILE):
        at = slice(n, n + TILE)
        high_o, low_o, live_o = high_r[:, at], low_r[:, at], live_r[:, at]
        cross = dot(high, high_o) + dot(low, high_o) + dot(high, low_o)
        sum_l = dot(high, live_o) + dot(low, live_o)
        square_l = dot(sq_high, live_o) + dot(sq_low, live_o)
        sum_r = dot(live, high_o) + dot(live, low_o)
        square_r = dot(live, sq_high_r[:, at]) + dot(live, sq_low_r[:, at])
        pairs = jnp.minimum(wide[1], own_last[:, at]) - jnp.maximum(wide[0], own_first[:, at])
        pairs = jnp.maximum(pairs, 1.0)
        covariance = pairs * cross - sum_l * sum_r
        var_l = jnp.maximum(pairs * square_l - sum_l * sum_l, pairs)
        var_r = jnp.maximum(pairs * square_r - sum_r * sum_r, pairs)
        out_ref[:, at] = covariance * lax.rsqrt(var_l * var_r)


def correlated(windows, listed_from, listed_until, whole):
    full = lambda *shape: pl.BlockSpec(shape, lambda g: (0,) * len(shape))
    return pl.pallas_call(
        correlate_kernel,
        grid=(ASSETS // ROWS,),
        out_shape=jax.ShapeDtypeStruct((ASSETS, COLS), F32),
        in_specs=[
            pl.BlockSpec(memory_space=pltpu.SMEM),
            full(1, ASSETS),
            full(1, ASSETS),
            full(NY, SPAN, COLS),
        ],
        out_specs=pl.BlockSpec((ROWS, COLS), lambda g: (g, 0)),
        scratch_shapes=[pltpu.VMEM((SPAN, COLS), BF16)] * 5,
        compiler_params=pltpu.CompilerParams(dimension_semantics=("arbitrary",), vmem_limit_bytes=16 << 20),
    )(windows, listed_from[None], listed_until[None], whole)


def on_device(returns, windows, listed_from, listed_until):
    whole = gathered(returns).reshape(NY, SPAN, COLS)
    return correlated(windows, listed_from, listed_until, whole)[None]


def solution(mesh):
    placed = (P("tm", "asset"), P("tm"), P(), P())
    return jax.shard_map(
        on_device, mesh=mesh, in_specs=placed, out_specs=P("tm", None, "asset"), check_vma=False
    )
```

time: 45.2 us -> 37.4 us (0.83)
  the two profiles are of different devices: /device:TPU:1 before, /device:TPU:65 now
where the time goes in v2:
time: 37.4 us; the launch traced here: 37.1 us
  Pallas kernels  34.3 us (92%)
  local copies, waits for them, and re-layouts  2.14 us (6%)
  between operations  0.68 us (2%)
    pallas_call x1, Pallas kernels, gathered(): pl.pallas_call(gather_kernel, out_shape=jax.ShapeDtypeStruct((NY, 2, 2, N...  23.9 us
    pallas_call x1, Pallas kernels, correlated(): pl.pallas_call(correlate_kernel, grid=(ASSETS // ROWS,), out_shape=jax.Sh...  10.4 us
    unnamed x6, local copies, waits for them, and re-layouts  2.14 us

profile of v2, /device:TPU:65, one launch (start us, length us, event | category | flops | bytes accessed | tf_op | source)
XLA Modules:
  0.0 37.1 jit_solution(17680530175279919775)
XLA Ops:
  0.7 0.0 copy-start
  0.7 0.7 %copy-done = f32[16,512]{1,0:T(8,128)S(1)} copy-done((f32[16,512]{1,0:T(8,128)S(1)}, f32[16,512]{1,0:T(8,128)}, u32[]{:S(2)}) %copy-start) | copy-done | bytes 32792
  1.4 23.9 %shard_map.46 = f32[4,2,2,4,2,8,512]{6,5,4,3,2,1,0:T(8,128)S(1)} custom-call(f32[16,512]{1,0:T(8,128)S(1)} %copy-done), custom_call_target="tpu_custom_call" | custom-call | tf_op jit(solution)/shard_map/pallas_call | solution.py:260
  25.3 0.0 copy-start.1
  25.3 0.7 %copy-done.1 = s32[2048]{0:T(1024)S(1)} copy-done((s32[2048]{0:T(1024)S(1)}, s32[2048]{0:T(1024)}, u32[]{:S(2)}) %copy-start.1) | copy-done | bytes 8216
  26.0 0.0 copy-start.2
  26.0 0.7 %copy-done.2 = s32[2048]{0:T(1024)S(1)} copy-done((s32[2048]{0:T(1024)S(1)}, s32[2048]{0:T(1024)}, u32[]{:S(2)}) %copy-start.2) | copy-done | bytes 8216
  26.7 10.4 %shard_map.47 = f32[2048,512]{1,0:T(8,128)} custom-call(s32[1]{0:T(128)S(6)} %copy.5.windows_ref, s32[1,2048]{1,0:T(1,128)S(1)} %bitcast.5, s32[1,2048]{1,0:T(1,128)S(1)} %bitcast.6, f32[4,256,512]{2,1,0:T(8,128)S(1)} %bitcast.4), custom_call_target="tpu_custom_call" | custom-call | tf_op jit(solution)/shard_map/pallas_call | solution.py:348
Async XLA Ops:
  0.7 0.8 %copy-start = (f32[16,512]{1,0:T(8,128)S(1)}, f32[16,512]{1,0:T(8,128)}, u32[]{:S(2)}) copy-start(f32[16,512]{1,0:T(8,128)} %returns_ref.1) | copy-start | bytes 98308
  25.3 0.7 %copy-start.1 = (s32[2048]{0:T(1024)S(1)}, s32[2048]{0:T(1024)}, u32[]{:S(2)}) copy-start(s32[2048]{0:T(1024)} %param.6) | copy-start | bytes 24580
  26.0 0.7 %copy-start.2 = (s32[2048]{0:T(1024)S(1)}, s32[2048]{0:T(1024)}, u32[]{:S(2)}) copy-start(s32[2048]{0:T(1024)} %param.7) | copy-start | bytes 24580

commit v3 on v2

v3 whole, which is shorter than its diff:
```python
import functools

import jax
import jax.numpy as jnp
from jax import lax
from jax.experimental import pallas as pl
from jax.experimental.pallas import tpu as pltpu
from jax.sharding import PartitionSpec as P

MESH = pl.DeviceIdType.MESH
F32, BF16 = jnp.float32, jnp.bfloat16
NZ, NX, NY = 8, 4, 4
GROUP, HALF, SPAN = 16, 8, 256
COLS, ASSETS = 512, 2048

Z_SEM = 0
YS_SEM = Z_SEM + 4
YSR_SEM = YS_SEM + 12
XA_SEM = YSR_SEM + 6
XAR_SEM = XA_SEM + 4
XB_SEM = XAR_SEM + 2
XBR_SEM = XB_SEM + 16
YA_SEM = XBR_SEM + 8
D_SEM = YA_SEM + 18
E_SEM = D_SEM + 4
N_SEM = E_SEM + 4


def gather_kernel(
    returns_ref,
    windows_ref,
    from_hbm,
    until_hbm,
    all_ref,
    own_ref,
    out_ref,
    from_ref,
    until_ref,
    back2,
    extra,
    wide_ref,
    ss,
    rs,
    local_sem,
):
    tm, y = lax.axis_index("tm"), lax.axis_index("asset")
    z, x, c = tm // 8, (tm // 2) % 4, tm % 2

    def dev(dz=0, dx=0, dy=0, dc=0):
        return (
            ((z + dz) % NZ) * 8 + ((x + dx) % NX) * 2 + (c + dc) % 2,
            (y + dy) % NY,
        )

    partner = dev(dc=1)

    def copy(src, dst, i, to):
        return pltpu.make_async_remote_copy(
            src_ref=src, dst_ref=dst, send_sem=ss.at[i], recv_sem=rs.at[i], device_id=to, device_id_type=MESH
        )

    def received(dst, i):
        copy(dst, dst, i, partner).wait_recv()

    def send(src, dst, i, to):
        copy(src, dst, i, to).start()

    def origin_block(h, at, k):
        return all_ref.at[at, c, h, x, k] if k < 2 else back2.at[h, at]

    loads = [
        pltpu.make_async_copy(returns_ref.at[pl.ds(h * HALF, HALF)], origin_block(h, y, 0), local_sem.at[h])
        for h in (0, 1)
    ]
    lists = [
        pltpu.make_async_copy(from_hbm, from_ref, local_sem.at[2]),
        pltpu.make_async_copy(until_hbm, until_ref, local_sem.at[3]),
    ]
    for load in loads + lists:
        load.start()
    barrier = pltpu.get_barrier_semaphore()

    def greet(peer):
        pl.semaphore_signal(barrier, inc=1, device_id=peer, device_id_type=MESH)

    flat = [dev(dx=1), dev(dx=-1), dev(dx=2), dev(dy=1), dev(dy=-1), dev(dy=2), partner]
    for k in (1, 2):
        pl.when(z >= k)(functools.partial(greet, dev(dz=-k)))
    for peer in flat:
        greet(peer)
    pl.semaphore_wait(barrier, len(flat) + jnp.minimum(NZ - 1 - z, 2))
    for load in loads:
        load.wait()

    step = (1, -1)

    def ring_x(dx):
        return (x + dx) % NX

    def z_send(h, k):
        @pl.when(z + k < NZ)
        def _():
            send(origin_block(h, y, 0), origin_block(h, y, k), Z_SEM + h * 2 + k - 1, dev(dz=k))

    def z_wait(k):
        @pl.when(z >= k)
        def _():
            for h in (0, 1):
                received(origin_block(h, y, k), Z_SEM + h * 2 + k - 1)

    def ys_send(k):
        for h in (0, 1):
            block = origin_block(h, y, k)
            for d in (0, 1):
                send(block, block, YS_SEM + h * 6 + k * 2 + d, dev(dy=step[d]))
            send(block, block, YSR_SEM + h * 3 + k, dev(dy=2))

    def ys_wait(k):
        for h in (1, 0):
            for d in (0, 1):
                received(origin_block(h, (y - step[d]) % NY, k), YS_SEM + h * 6 + k * 2 + d)

    def ysr_wait(k):
        for h in (1, 0):
            received(origin_block(h, (y + 2) % NY, k), YSR_SEM + h * 3 + k)

    def x_sem(h, j, d, slot):
        near, far = (XA_SEM, XAR_SEM) if h == 0 else (XB_SEM + j * 4, XBR_SEM + j * 2)
        return far + slot if d == 2 else near + d * 2 + slot

    def with_slot(k, up, go):
        if k == 1:
            go(up.astype(jnp.int32))
        elif k == 0:
            pl.when(up)(functools.partial(go, 0))
        else:
            pl.when(jnp.logical_not(up))(functools.partial(go, 1))

    def x_send(h, j, k):
        at = (y + j) % NY
        for d, dx in ((2, 2), (0, 1), (1, -1)):

            def go(slot, d=d, dx=dx):
                send(origin_block(h, at, k), all_ref.at[at, c, h, x, slot], x_sem(h, j, d, slot), dev(dx=dx))

            with_slot(k, ring_x(dx) > x, go)

    def x_wait(h, j, k, far, then=None):
        at = (y + j) % NY
        for d, dx in ((2, 2),) if far else ((0, 1), (1, -1)):

            def go(slot, d=d, dx=dx):
                received(all_ref.at[at, c, h, ring_x(-dx), slot], x_sem(h, j, d, slot))
                if then is not None:
                    then(dx % NX, slot)

            with_slot(k, ring_x(-dx) < x, go)

    def ya_send(dist, slot):
        view = all_ref.at[y, c, 0, ring_x(-dist), slot]
        for dy in (2, 1, 3):
            send(view, view, YA_SEM + (dist - 1) * 6 + (dy - 1) * 2 + slot, dev(dy=dy))

    def ya_wait(j):
        for dist in (1, 3, 2):
            for slot in (0, 1):
                view = all_ref.at[(y + j) % NY, c, 0, ring_x(-dist), slot]
                received(view, YA_SEM + (dist - 1) * 6 + (3 - j) * 2 + slot)

    def x_all(h, j, ks=(0, 1, 2)):
        for k in ks:
            for far in (False, True):
                x_wait(h, j, k, far)

    def to_partner(j):
        at = (y + j) % NY
        send(all_ref.at[at, c], all_ref.at[at, c], D_SEM + j, partner)

        @pl.when(c == 1)
        def _():
            send(back2.at[:, at], extra.at[:, at], E_SEM + j, partner)

    def from_partner(j):
        at = (y + j) % NY
        received(all_ref.at[at, 1 - c], D_SEM + j)

        @pl.when(c == 0)
        def _():
            received(extra.at[:, at], E_SEM + j)
            all_ref[at, 1, :, x, 0] = extra[:, at]

    for k in (2, 1):
        for h in (1, 0):
            z_send(h, k)
    ys_send(0)
    x_send(0, 0, 0)
    x_send(1, 0, 0)
    ys_wait(0)
    x_send(1, 1, 0)
    x_send(1, 3, 0)
    z_wait(1)
    x_send(0, 0, 1)
    ys_send(1)
    x_send(1, 0, 1)
    ysr_wait(0)
    x_send(1, 2, 0)
    z_wait(2)
    x_send(0, 0, 2)
    ys_send(2)
    x_send(1, 0, 2)
    x_wait(0, 0, 0, False, ya_send)
    x_wait(0, 0, 0, True, ya_send)
    ys_wait(1)
    x_send(1, 1, 1)
    x_send(1, 3, 1)
    x_wait(0, 0, 1, False, ya_send)
    ysr_wait(1)
    x_send(1, 2, 1)
    x_wait(0, 0, 1, True, ya_send)
    ys_wait(2)
    x_send(1, 1, 2)
    x_send(1, 3, 2)
    x_wait(0, 0, 2, False, ya_send)
    ysr_wait(2)
    x_send(1, 2, 2)
    x_wait(0, 0, 2, True, ya_send)
    x_all(1, 0)
    to_partner(0)
    from_partner(0)

    for load in lists:
        load.wait()
    spans = spans_of(windows_ref, from_ref, until_ref, tm)
    own_spans = spans(pl.multiple_of(y * COLS, COLS), COLS)
    prepare_own(all_ref[y].reshape(SPAN, COLS), own_spans, tm, own_ref)

    def own_rows(i):
        at = pl.multiple_of(y * COLS + i * ROWS, ROWS)
        raw = all_ref[y].reshape(SPAN, COLS)[:, i * ROWS : (i + 1) * ROWS]
        rows = prepare(raw, spans(at, ROWS), tm, wide_ref)
        correlate(wide_ref, rows, own_ref, own_spans, out_ref.at[pl.ds(i * ROWS, ROWS)])

    own_rows(0)
    for j in (1, 3, 2):
        x_all(1, j)
        ya_wait(j)
        to_partner(j)
    own_rows(1)
    for j in (1, 3, 2):
        from_partner(j)

    block, many = back2.at[0, 0], all_ref.at[0, 0]
    for i in range(E_SEM):
        view = many if i >= D_SEM else block
        done = copy(view, view, i, partner).wait_send
        if i < YS_SEM:
            pl.when(z + 1 + i % 2 < NZ)(done)
        else:
            done()

    @pl.when(c == 1)
    def _():
        for j in range(4):
            copy(back2.at[:, 0], extra.at[:, 0], E_SEM + j, partner).wait_send()


ROWS = 256
TILE = 256


def day_of(row, tm):
    core, half, at, slot, day = row // 128, (row // 64) % 2, (row // 16) % 4, (row // 8) % 2, row % 8
    place = at * 2 + core
    later = (at > (tm // 2) % 4).astype(jnp.int32)
    back = jnp.where((place == tm % 8 + 1) & (core == 1), 2 - slot, slot + later)
    return ((tm // 8 - back) * 8 + place) * GROUP + half * HALF + day


def split(value):
    high = value.astype(BF16)
    return high, (value - high.astype(F32)).astype(BF16)


def dot(left, right):
    return jnp.dot(left, right, preferred_element_type=F32)


def spans_of(windows_ref, from_ref, until_ref, tm):
    end = (tm + 1) * GROUP
    begin = jnp.maximum(end - windows_ref[0], 0)

    def spans(at, width):
        first = jnp.maximum(from_ref[:, pl.ds(at, width)], begin).astype(F32)
        last = jnp.minimum(until_ref[:, pl.ds(at, width)], end).astype(F32)
        return first, last

    return spans


def terms(day, first, last, raw, out_ref):
    live = (day >= first) & (day < last)
    value = jnp.where(live, raw, 0.0)
    out_ref[0] = live.astype(F32).astype(BF16)
    out_ref[1], out_ref[2] = split(value)
    out_ref[3], out_ref[4] = split(value * value)


def prepare_own(raw, spans, tm, own_ref):
    day = day_of(lax.broadcasted_iota(jnp.int32, (SPAN, 128), 0), tm).astype(F32)
    for n in range(0, COLS, 128):
        at = slice(n, n + 128)
        terms(day, spans[0][:, at], spans[1][:, at], raw[:, at], own_ref.at[:, :, pl.ds(n, 128)])


def prepare(raw, spans, tm, wide_ref):
    day = day_of(lax.broadcasted_iota(jnp.int32, (1, SPAN), 1), tm).astype(F32)
    first, last = (jnp.broadcast_to(span, (128, ROWS)).T for span in spans)
    for n in range(0, SPAN, 128):
        terms(day[:, n : n + 128], first, last, raw[n : n + 128].T, wide_ref.at[:, :, pl.ds(n, 128)])
    return first, last


def correlate(wide, rows, own_ref, own_spans, out_ref):
    first, last = rows
    live, high, low, sq_high, sq_low = (wide[i] for i in range(5))
    for n in range(0, COLS, TILE):
        at = slice(n, n + TILE)
        live_o, high_o, low_o, sq_high_o, sq_low_o = (own_ref[i, :, at] for i in range(5))
        cross = dot(high, high_o) + dot(low, high_o) + dot(high, low_o)
        sum_l = dot(high, live_o) + dot(low, live_o)
        square_l = dot(sq_high, live_o) + dot(sq_low, live_o)
        sum_r = dot(live, high_o) + dot(live, low_o)
        square_r = dot(live, sq_high_o) + dot(live, sq_low_o)
        pairs = jnp.concatenate(
            [
                jnp.minimum(last, own_spans[1][:, m : m + 128]) - jnp.maximum(first, own_spans[0][:, m : m + 128])
                for m in range(n, n + TILE, 128)
            ],
            axis=1,
        )
        pairs = jnp.maximum(pairs, 1.0)
        covariance = pairs * cross - sum_l * sum_r
        var_l = jnp.maximum(pairs * square_l - sum_l * sum_l, pairs)
        var_r = jnp.maximum(pairs * square_r - sum_r * sum_r, pairs)
        out_ref[:, at] = covariance * lax.rsqrt(var_l * var_r)


def gathered(returns, windows, listed_from, listed_until):
    vmem, smem, hbm = (pl.BlockSpec(memory_space=space) for space in (pltpu.VMEM, pltpu.SMEM, pltpu.HBM))
    returns, listed_from, listed_until = (
        pltpu.with_memory_space_constraint(array, pltpu.HBM) for array in (returns, listed_from, listed_until)
    )
    return pl.pallas_call(
        gather_kernel,
        out_shape=[
            jax.ShapeDtypeStruct((NY, 2, 2, NX, 2, HALF, COLS), F32),
            jax.ShapeDtypeStruct((5, SPAN, COLS), BF16),
            jax.ShapeDtypeStruct((COLS, COLS), F32),
            jax.ShapeDtypeStruct((1, ASSETS), jnp.int32),
            jax.ShapeDtypeStruct((1, ASSETS), jnp.int32),
        ],
        in_specs=[hbm, smem, hbm, hbm],
        out_specs=[vmem] * 5,
        scratch_shapes=[
            pltpu.VMEM((2, NY, HALF, COLS), F32),
            pltpu.VMEM((2, NY, HALF, COLS), F32),
            pltpu.VMEM((5, ROWS, SPAN), BF16),
            pltpu.SemaphoreType.DMA((N_SEM,)),
            pltpu.SemaphoreType.DMA((N_SEM,)),
            pltpu.SemaphoreType.DMA((4,)),
        ],
        compiler_params=pltpu.CompilerParams(collective_id=0, has_side_effects=True, vmem_limit_bytes=16 << 20),
    )(returns, windows, listed_from, listed_until)


ORDER = (1, 3, 2)


def rest_kernel(windows_ref, all_ref, own_ref, done_ref, from_ref, until_ref, out_ref, wide_a, wide_b, result, sems):
    tm, y = lax.axis_index("tm"), lax.axis_index("asset")
    spans = spans_of(windows_ref, from_ref, until_ref, tm)
    own_spans = spans(pl.multiple_of(y * COLS, COLS), COLS)
    copies = [pltpu.make_async_copy(done_ref, out_ref.at[pl.ds(pl.multiple_of(y * COLS, COLS), COLS)], sems.at[6])]
    copies[0].start()
    wides = wide_a, wide_b

    def place(i):
        at = (y + ORDER[i // 2]) % NY
        return at, pl.multiple_of(at * COLS + (i % 2) * ROWS, ROWS)

    def ready(i):
        at, row = place(i)
        raw = all_ref[at].reshape(SPAN, COLS)[:, (i % 2) * ROWS : (i % 2 + 1) * ROWS]
        return prepare(raw, spans(row, ROWS), tm, wides[i % 2])

    rows = ready(0)
    for i in range(6):
        now = rows
        if i < 5:
            rows = ready(i + 1)
        correlate(wides[i % 2], now, own_ref, own_spans, result.at[i])
        copies.append(pltpu.make_async_copy(result.at[i], out_ref.at[pl.ds(place(i)[1], ROWS)], sems.at[i]))
        copies[-1].start()
    for copy in copies:
        copy.wait()


def completed(windows, whole, own, done, listed_from, listed_until):
    vmem, smem = pl.BlockSpec(memory_space=pltpu.VMEM), pl.BlockSpec(memory_space=pltpu.SMEM)
    return pl.pallas_call(
        rest_kernel,
        out_shape=jax.ShapeDtypeStruct((ASSETS, COLS), F32),
        in_specs=[smem, vmem, vmem, vmem, vmem, vmem],
        out_specs=pl.BlockSpec(memory_space=pltpu.HBM),
        scratch_shapes=[pltpu.VMEM((5, ROWS, SPAN), BF16)] * 2
        + [pltpu.VMEM((6, ROWS, COLS), F32), pltpu.SemaphoreType.DMA((7,))],
        compiler_params=pltpu.CompilerParams(vmem_limit_bytes=20 << 20),
    )(windows, whole, own, done, listed_from, listed_until)


def on_device(returns, windows, listed_from, listed_until):
    return completed(windows, *gathered(returns, windows, listed_from[None], listed_until[None]))[None]


def solution(mesh):
    placed = (P("tm", "asset"), P("tm"), P(), P())
    return jax.shard_map(
        on_device, mesh=mesh, in_specs=placed, out_specs=P("tm", None, "asset"), check_vma=False
    )
```

time: 37.4 us -> 31.1 us (0.83)
  Pallas kernels: 34.3 us -> 30.3 us
  local copies, waits for them, and re-layouts: 2.14 us -> 0 us
    pallas_call x2, Pallas kernels: 34.3 us -> 30.3 us  [the longest x1 23.7 us: gathered(): pl.pallas_call(gather_kernel, out_shape=[jax.ShapeDtypeStruct((NY, 2, 2,...]
    unnamed x6 -> x0, local copies, waits for them, and re-layouts: 2.14 us -> none
where the time goes in v3:
time: 31.1 us; the launch traced here: 31 us
  Pallas kernels  30.3 us (97%)
  between operations  0.66 us (2%)
    pallas_call x1, Pallas kernels, gathered(): pl.pallas_call(gather_kernel, out_shape=[jax.ShapeDtypeStruct((NY, 2, 2,...  23.7 us
    pallas_call x1, Pallas kernels, completed(): pl.pallas_call(rest_kernel, out_shape=jax.ShapeDtypeStruct((ASSETS, COLS)...  6.57 us

profile of v3, /device:TPU:65, one launch (start us, length us, event | category | flops | bytes accessed | tf_op | source)
XLA Modules:
  0.0 31.0 jit_solution(2705829494033395618)
XLA Ops:
  0.7 23.7 %shard_map.46 = (f32[4,2,2,4,2,8,512]{6,5,4,3,2,1,0:T(8,128)S(1)}, bf16[5,256,512]{2,1,0:T(8,128)(2,1)S(1)}, f32[512,512]{1,0:T(8,128)S(1)}, s32[1,2048]{1,0:T(1,128)S(1)}, s32[1,2048]{1,0:T(1,128)S(1)}) custom-call(f32[16,512]{1,0:T(8,128)} %returns_ref.1, s32[1]{0:T(128)S(6)} %copy.5.windows_ref, s32[1,2048]{1,0:T(1,128)} %bitcast.3, s32[1,2048]{1,0:T(1,128)} %bitcast.4), custom_call_target="tpu_custom_call" | custom-call | tf_op jit(solution)/shard_map/pallas_call | solution.py:353
  24.4 6.6 %shard_map.47 = f32[2048,512]{1,0:T(8,128)} custom-call(s32[1]{0:T(128)S(6)} %copy.5.windows_ref, f32[4,2,2,4,2,8,512]{6,5,4,3,2,1,0:T(8,128)S(1)} %get-tuple-element.10.all_ref, bf16[5,256,512]{2,1,0:T(8,128)(2,1)S(1)} %get-tuple-element.11.own_ref, f32[512,512]{1,0:T(8,128)S(1)} %get-tuple-element.12.done_ref, s32[1,2048]{1,0:T(1,128)S(1)} %get-tuple-element.13.from_ref, ...), custom_call_target="tpu_custom_call" | custom-call | tf_op jit(solution)/shard_map/pallas_call | solution.py:410

commit v4 on v3

--- a/solution.py
+++ b/solution.py
@@ -108,21 +108,37 @@
             for h in (0, 1):
                 received(origin_block(h, y, k), Z_SEM + h * 2 + k - 1)
 
-    def ys_send(k):
-        for h in (0, 1):
-            block = origin_block(h, y, k)
-            for d in (0, 1):
-                send(block, block, YS_SEM + h * 6 + k * 2 + d, dev(dy=step[d]))
-            send(block, block, YSR_SEM + h * 3 + k, dev(dy=2))
-
-    def ys_wait(k):
+    def y_sem(h, j, k):
+        return YSR_SEM + h * 3 + k if j == 2 else YS_SEM + h * 6 + k * 2 + (0 if j == 3 else 1)
+
+    def ys_send(js):
         for h in (1, 0):
-            for d in (0, 1):
-                received(origin_block(h, (y - step[d]) % NY, k), YS_SEM + h * 6 + k * 2 + d)
-
-    def ysr_wait(k):
-        for h in (1, 0):
-            received(origin_block(h, (y + 2) % NY, k), YSR_SEM + h * 3 + k)
+            block = origin_block(h, y, 0)
+            for j in js:
+                send(block, block, y_sem(h, (NY - j) % NY, 0), dev(dy=j))
+
+    def needed(h, k):
+        return (z >= k) & (c == 1) if (h, k) == (0, 2) else z >= k
+
+    def passed_on(h, k):
+        here = (z >= k - 1) & (z + 1 < NZ)
+        return here & (c == 1) if (h, k) == (0, 2) else here
+
+    def ys_wait(js, k):
+        for j in js:
+            at = (y + j) % NY
+            for h in (1, 0):
+
+                def arrive(h=h, at=at, j=j):
+                    received(origin_block(h, at, k), y_sem(h, j, k))
+
+                arrive() if k == 0 else pl.when(needed(h, k))(arrive)
+
+                def forward(h=h, at=at, j=j):
+                    send(origin_block(h, at, k), origin_block(h, at, k + 1), y_sem(h, j, k + 1), dev(dz=1))
+
+                if k < 2:
+                    pl.when(passed_on(h, k + 1))(forward)
 
     def x_sem(h, j, d, slot):
         near, far = (XA_SEM, XAR_SEM) if h == 0 else (XB_SEM + j * 4, XBR_SEM + j * 2)
@@ -156,9 +172,9 @@
 
             with_slot(k, ring_x(-dx) < x, go)
 
-    def ya_send(dist, slot):
+    def ya_send(dist, slot, to=(1, 3)):
         view = all_ref.at[y, c, 0, ring_x(-dist), slot]
-        for dy in (2, 1, 3):
+        for dy in to:
             send(view, view, YA_SEM + (dist - 1) * 6 + (dy - 1) * 2 + slot, dev(dy=dy))
 
     def ya_wait(j):
@@ -189,72 +205,80 @@
             received(extra.at[:, at], E_SEM + j)
             all_ref[at, 1, :, x, 0] = extra[:, at]
 
+    ys_send((1, 3, 2))
     for k in (2, 1):
         for h in (1, 0):
             z_send(h, k)
-    ys_send(0)
-    x_send(0, 0, 0)
-    x_send(1, 0, 0)
-    ys_wait(0)
+    for k in (0, 1, 2):
+        if k:
+            z_wait(k)
+        x_send(0, 0, k)
+        x_send(1, 0, k)
+    ys_wait((1, 3), 0)
     x_send(1, 1, 0)
     x_send(1, 3, 0)
-    z_wait(1)
-    x_send(0, 0, 1)
-    ys_send(1)
-    x_send(1, 0, 1)
-    ysr_wait(0)
-    x_send(1, 2, 0)
-    z_wait(2)
-    x_send(0, 0, 2)
-    ys_send(2)
-    x_send(1, 0, 2)
-    x_wait(0, 0, 0, False, ya_send)
-    x_wait(0, 0, 0, True, ya_send)
-    ys_wait(1)
+    ys_wait((2,), 0)
+    for k in (0, 1):
+        x_wait(0, 0, k, False, ya_send)
+        x_wait(0, 0, k, True, ya_send)
+    ys_wait((1, 3), 1)
     x_send(1, 1, 1)
     x_send(1, 3, 1)
-    x_wait(0, 0, 1, False, ya_send)
-    ysr_wait(1)
-    x_send(1, 2, 1)
-    x_wait(0, 0, 1, True, ya_send)
-    ys_wait(2)
+    ys_wait((2,), 1)
+    x_wait(0, 0, 2, False, ya_send)
+    x_wait(0, 0, 2, True, ya_send)
+    ys_wait((1, 3), 2)
     x_send(1, 1, 2)
     x_send(1, 3, 2)
-    x_wait(0, 0, 2, False, ya_send)
-    ysr_wait(2)
+    for dist in (1, 3, 2):
+        for slot in (0, 1):
+            ya_send(dist, slot, (2,))
+    x_send(1, 2, 0)
+    x_send(1, 2, 1)
+    ys_wait((2,), 2)
     x_send(1, 2, 2)
-    x_wait(0, 0, 2, True, ya_send)
     x_all(1, 0)
     to_partner(0)
-    from_partner(0)
 
     for load in lists:
         load.wait()
     spans = spans_of(windows_ref, from_ref, until_ref, tm)
     own_spans = spans(pl.multiple_of(y * COLS, COLS), COLS)
+
+    def some_rows(i):
+        at, row = place_of(i, y)
+        raw = all_ref[at].reshape(SPAN, COLS)[:, (i % 2) * ROWS : (i % 2 + 1) * ROWS]
+        rows = prepare(raw, spans(row, ROWS), tm, wide_ref)
+        correlate(wide_ref, rows, own_ref, own_spans, out_ref.at[pl.ds(i * ROWS, ROWS)])
+
+    from_partner(0)
     prepare_own(all_ref[y].reshape(SPAN, COLS), own_spans, tm, own_ref)
-
-    def own_rows(i):
-        at = pl.multiple_of(y * COLS + i * ROWS, ROWS)
-        raw = all_ref[y].reshape(SPAN, COLS)[:, i * ROWS : (i + 1) * ROWS]
-        rows = prepare(raw, spans(at, ROWS), tm, wide_ref)
-        correlate(wide_ref, rows, own_ref, own_spans, out_ref.at[pl.ds(i * ROWS, ROWS)])
-
-    own_rows(0)
-    for j in (1, 3, 2):
-        x_all(1, j)
-        ya_wait(j)
-        to_partner(j)
-    own_rows(1)
-    for j in (1, 3, 2):
-        from_partner(j)
-
+    some_rows(0)
+    some_rows(1)
+    x_all(1, 1)
+    ya_wait(1)
+    to_partner(1)
+    x_all(1, 3)
+    ya_wait(3)
+    to_partner(3)
+    from_partner(1)
+    some_rows(2)
+    x_all(1, 2)
+    ya_wait(2)
+    to_partner(2)
+    some_rows(3)
+    from_partner(3)
+    some_rows(4)
+    from_partner(2)
     block, many = back2.at[0, 0], all_ref.at[0, 0]
     for i in range(E_SEM):
         view = many if i >= D_SEM else block
         done = copy(view, view, i, partner).wait_send
         if i < YS_SEM:
             pl.when(z + 1 + i % 2 < NZ)(done)
+        elif i < XA_SEM:
+            h, k = divmod(i - YSR_SEM, 3) if i >= YSR_SEM else divmod((i - YS_SEM) // 2, 3)
+            pl.when(passed_on(h, k))(done) if k else done()
         else:
             done()
 
@@ -266,6 +290,13 @@
 
 ROWS = 256
 TILE = 256
+ORDER = (0, 1, 3, 2)
+FIRST = 5
+
+
+def place_of(i, y):
+    at = (y + ORDER[i // 2]) % NY
+    return at, pl.multiple_of(at * COLS + (i % 2) * ROWS, ROWS)
 
 
 def day_of(row, tm):
@@ -355,7 +386,7 @@
         out_shape=[
             jax.ShapeDtypeStruct((NY, 2, 2, NX, 2, HALF, COLS), F32),
             jax.ShapeDtypeStruct((5, SPAN, COLS), BF16),
-            jax.ShapeDtypeStruct((COLS, COLS), F32),
+            jax.ShapeDtypeStruct((FIRST * ROWS, COLS), F32),
             jax.ShapeDtypeStruct((1, ASSETS), jnp.int32),
             jax.ShapeDtypeStruct((1, ASSETS), jnp.int32),
         ],
@@ -373,34 +404,32 @@
     )(returns, windows, listed_from, listed_until)
 
 
-ORDER = (1, 3, 2)
-
-
 def rest_kernel(windows_ref, all_ref, own_ref, done_ref, from_ref, until_ref, out_ref, wide_a, wide_b, result, sems):
     tm, y = lax.axis_index("tm"), lax.axis_index("asset")
     spans = spans_of(windows_ref, from_ref, until_ref, tm)
     own_spans = spans(pl.multiple_of(y * COLS, COLS), COLS)
-    copies = [pltpu.make_async_copy(done_ref, out_ref.at[pl.ds(pl.multiple_of(y * COLS, COLS), COLS)], sems.at[6])]
-    copies[0].start()
+    copies = []
+
+    def store(src, i):
+        copies.append(pltpu.make_async_copy(src, out_ref.at[pl.ds(place_of(i, y)[1], ROWS)], sems.at[i]))
+        copies[-1].start()
+
+    for i in range(FIRST):
+        store(done_ref.at[pl.ds(i * ROWS, ROWS)], i)
     wides = wide_a, wide_b
 
-    def place(i):
-        at = (y + ORDER[i // 2]) % NY
-        return at, pl.multiple_of(at * COLS + (i % 2) * ROWS, ROWS)
-
     def ready(i):
-        at, row = place(i)
+        at, row = place_of(i, y)
         raw = all_ref[at].reshape(SPAN, COLS)[:, (i % 2) * ROWS : (i % 2 + 1) * ROWS]
         return prepare(raw, spans(row, ROWS), tm, wides[i % 2])
 
-    rows = ready(0)
-    for i in range(6):
+    rows = ready(FIRST)
+    for i in range(FIRST, 8):
         now = rows
-        if i < 5:
+        if i < 7:
             rows = ready(i + 1)
-        correlate(wides[i % 2], now, own_ref, own_spans, result.at[i])
-        copies.append(pltpu.make_async_copy(result.at[i], out_ref.at[pl.ds(place(i)[1], ROWS)], sems.at[i]))
-        copies[-1].start()
+        correlate(wides[i % 2], now, own_ref, own_spans, result.at[i - FIRST])
+        store(result.at[i - FIRST], i)
     for copy in copies:
         copy.wait()
 
@@ -413,7 +442,7 @@
         in_specs=[smem, vmem, vmem, vmem, vmem, vmem],
         out_specs=pl.BlockSpec(memory_space=pltpu.HBM),
         scratch_shapes=[pltpu.VMEM((5, ROWS, SPAN), BF16)] * 2
-        + [pltpu.VMEM((6, ROWS, COLS), F32), pltpu.SemaphoreType.DMA((7,))],
+        + [pltpu.VMEM((8 - FIRST, ROWS, COLS), F32), pltpu.SemaphoreType.DMA((8,))],
         compiler_params=pltpu.CompilerParams(vmem_limit_bytes=20 << 20),
     )(windows, whole, own, done, listed_from, listed_until)
 

time: 31.1 us -> 29.5 us (0.949)
  the two profiles are of different devices: /device:TPU:65 before, /device:TPU:120 now
where the time goes in v4:
time: 29.5 us; the launch traced here: 29.4 us
  Pallas kernels  28.7 us (97%)
  between operations  0.66 us (2%)
    pallas_call x1, Pallas kernels, gathered(): pl.pallas_call(gather_kernel, out_shape=[jax.ShapeDtypeStruct((NY, 2, 2,...  24.9 us
    pallas_call x1, Pallas kernels, completed(): pl.pallas_call(rest_kernel, out_shape=jax.ShapeDtypeStruct((ASSETS, COLS)...  3.83 us

profile of v4, /device:TPU:120, one launch (start us, length us, event | category | flops | bytes accessed | tf_op | source)
XLA Modules:
  0.0 29.4 jit_solution(4978363834061478309)
XLA Ops:
  0.7 24.9 %shard_map.46 = (f32[4,2,2,4,2,8,512]{6,5,4,3,2,1,0:T(8,128)S(1)}, bf16[5,256,512]{2,1,0:T(8,128)(2,1)S(1)}, f32[1280,512]{1,0:T(8,128)S(1)}, s32[1,2048]{1,0:T(1,128)S(1)}, s32[1,2048]{1,0:T(1,128)S(1)}) custom-call(f32[16,512]{1,0:T(8,128)} %returns_ref.1, s32[1]{0:T(128)S(6)} %copy.5.windows_ref, s32[1,2048]{1,0:T(1,128)} %bitcast.3, s32[1,2048]{1,0:T(1,128)} %bitcast.4), custom_call_target="tpu_custom_call" | custom-call | tf_op jit(solution)/shard_map/pallas_call | solution.py:384
  25.6 3.8 %shard_map.47 = f32[2048,512]{1,0:T(8,128)} custom-call(s32[1]{0:T(128)S(6)} %copy.5.windows_ref, f32[4,2,2,4,2,8,512]{6,5,4,3,2,1,0:T(8,128)S(1)} %get-tuple-element.10.all_ref, bf16[5,256,512]{2,1,0:T(8,128)(2,1)S(1)} %get-tuple-element.11.own_ref, f32[1280,512]{1,0:T(8,128)S(1)} %get-tuple-element.12.done_ref, s32[1,2048]{1,0:T(1,128)S(1)} %get-tuple-element.13.from_ref, ...), custom_call_target="tpu_custom_call" | custom-call | tf_op jit(solution)/shard_map/pallas_call | solution.py:439

commit v5 on v4

--- a/solution.py
+++ b/solution.py
@@ -89,7 +89,7 @@
     for peer in flat:
         greet(peer)
     pl.semaphore_wait(barrier, len(flat) + jnp.minimum(NZ - 1 - z, 2))
-    for load in loads:
+    for load in loads + lists:
         load.wait()
 
     step = (1, -1)
@@ -111,34 +111,27 @@
     def y_sem(h, j, k):
         return YSR_SEM + h * 3 + k if j == 2 else YS_SEM + h * 6 + k * 2 + (0 if j == 3 else 1)
 
-    def ys_send(js):
-        for h in (1, 0):
-            block = origin_block(h, y, 0)
-            for j in js:
-                send(block, block, y_sem(h, (NY - j) % NY, 0), dev(dy=j))
-
     def needed(h, k):
         return (z >= k) & (c == 1) if (h, k) == (0, 2) else z >= k
 
-    def passed_on(h, k):
-        here = (z >= k - 1) & (z + 1 < NZ)
-        return here & (c == 1) if (h, k) == (0, 2) else here
+    def when_needed(h, k, go):
+        go() if k == 0 else pl.when(needed(h, k))(go)
+
+    def ys_send(js, k):
+        for h in (1, 0):
+            for j in js:
+                block = origin_block(h, y, k)
+                when_needed(h, k, functools.partial(send, block, block, y_sem(h, (NY - j) % NY, k), dev(dy=j)))
 
     def ys_wait(js, k):
         for j in js:
             at = (y + j) % NY
             for h in (1, 0):
-
-                def arrive(h=h, at=at, j=j):
-                    received(origin_block(h, at, k), y_sem(h, j, k))
-
-                arrive() if k == 0 else pl.when(needed(h, k))(arrive)
-
-                def forward(h=h, at=at, j=j):
-                    send(origin_block(h, at, k), origin_block(h, at, k + 1), y_sem(h, j, k + 1), dev(dz=1))
-
-                if k < 2:
-                    pl.when(passed_on(h, k + 1))(forward)
+                block = origin_block(h, at, k)
+                when_needed(h, k, functools.partial(received, block, y_sem(h, j, k)))
+                if k == 0:
+                    above = functools.partial(send, block, origin_block(h, at, 1), y_sem(h, j, 1), dev(dz=1))
+                    pl.when(z + 1 < NZ)(above)
 
     def x_sem(h, j, d, slot):
         near, far = (XA_SEM, XAR_SEM) if h == 0 else (XB_SEM + j * 4, XBR_SEM + j * 2)
@@ -205,51 +198,53 @@
             received(extra.at[:, at], E_SEM + j)
             all_ref[at, 1, :, x, 0] = extra[:, at]
 
-    ys_send((1, 3, 2))
+    spans = spans_of(windows_ref, from_ref, until_ref, tm)
+    own_spans = spans(pl.multiple_of(y * COLS, COLS), COLS)
+
+    def some_rows(i):
+        at, row = place_of(i, y)
+        raw = all_ref[at].reshape(SPAN, COLS)[:, (i % 2) * ROWS : (i % 2 + 1) * ROWS]
+        rows = prepare(raw, spans(row, ROWS), tm, wide_ref)
+        correlate(wide_ref, rows, own_ref, own_spans, out_ref.at[pl.ds(i * ROWS, ROWS)])
+
     for k in (2, 1):
         for h in (1, 0):
             z_send(h, k)
-    for k in (0, 1, 2):
-        if k:
-            z_wait(k)
-        x_send(0, 0, k)
-        x_send(1, 0, k)
+    ys_send((2, 1, 3), 0)
+    x_send(0, 0, 0)
+    x_send(1, 0, 0)
+    z_wait(1)
+    x_send(0, 0, 1)
+    x_send(1, 0, 1)
+    z_wait(2)
+    ys_send((2, 1, 3), 2)
+    x_send(0, 0, 2)
+    x_send(1, 0, 2)
     ys_wait((1, 3), 0)
     x_send(1, 1, 0)
     x_send(1, 3, 0)
     ys_wait((2,), 0)
+    x_send(1, 2, 0)
     for k in (0, 1):
         x_wait(0, 0, k, False, ya_send)
         x_wait(0, 0, k, True, ya_send)
     ys_wait((1, 3), 1)
     x_send(1, 1, 1)
     x_send(1, 3, 1)
-    ys_wait((2,), 1)
-    x_wait(0, 0, 2, False, ya_send)
-    x_wait(0, 0, 2, True, ya_send)
     ys_wait((1, 3), 2)
     x_send(1, 1, 2)
     x_send(1, 3, 2)
+    ys_wait((2,), 2)
+    x_send(1, 2, 2)
+    x_wait(0, 0, 2, False, ya_send)
+    x_wait(0, 0, 2, True, ya_send)
     for dist in (1, 3, 2):
         for slot in (0, 1):
             ya_send(dist, slot, (2,))
-    x_send(1, 2, 0)
+    ys_wait((2,), 1)
     x_send(1, 2, 1)
-    ys_wait((2,), 2)
-    x_send(1, 2, 2)
     x_all(1, 0)
     to_partner(0)
-
-    for load in lists:
-        load.wait()
-    spans = spans_of(windows_ref, from_ref, until_ref, tm)
-    own_spans = spans(pl.multiple_of(y * COLS, COLS), COLS)
-
-    def some_rows(i):
-        at, row = place_of(i, y)
-        raw = all_ref[at].reshape(SPAN, COLS)[:, (i % 2) * ROWS : (i % 2 + 1) * ROWS]
-        rows = prepare(raw, spans(row, ROWS), tm, wide_ref)
-        correlate(wide_ref, rows, own_ref, own_spans, out_ref.at[pl.ds(i * ROWS, ROWS)])
 
     from_partner(0)
     prepare_own(all_ref[y].reshape(SPAN, COLS), own_spans, tm, own_ref)
@@ -261,14 +256,15 @@
     x_all(1, 3)
     ya_wait(3)
     to_partner(3)
-    from_partner(1)
-    some_rows(2)
     x_all(1, 2)
     ya_wait(2)
     to_partner(2)
+    from_partner(1)
+    some_rows(2)
     some_rows(3)
     from_partner(3)
     some_rows(4)
+    some_rows(5)
     from_partner(2)
     block, many = back2.at[0, 0], all_ref.at[0, 0]
     for i in range(E_SEM):
@@ -278,7 +274,7 @@
             pl.when(z + 1 + i % 2 < NZ)(done)
         elif i < XA_SEM:
             h, k = divmod(i - YSR_SEM, 3) if i >= YSR_SEM else divmod((i - YS_SEM) // 2, 3)
-            pl.when(passed_on(h, k))(done) if k else done()
+            pl.when(z + 1 < NZ)(done) if k == 1 else when_needed(h, k, done)
         else:
             done()
 
@@ -291,7 +287,7 @@
 ROWS = 256
 TILE = 256
 ORDER = (0, 1, 3, 2)
-FIRST = 5
+FIRST = 6
 
 
 def place_of(i, y):

time: 29.5 us -> 28.8 us (0.976)
  Pallas kernels: 28.7 us -> 28.1 us
    pallas_call x1, Pallas kernels: 3.83 us -> 2.95 us  [completed(): pl.pallas_call(rest_kernel, out_shape=jax.ShapeDtypeStruct((ASSETS, COLS)...]
where the time goes in v5:
time: 28.8 us; the launch traced here: 28.7 us
  Pallas kernels  28.1 us (98%)
  between operations  0.66 us (2%)
    pallas_call x1, Pallas kernels, gathered(): pl.pallas_call(gather_kernel, out_shape=[jax.ShapeDtypeStruct((NY, 2, 2,...  25.1 us
    pallas_call x1, Pallas kernels, completed(): pl.pallas_call(rest_kernel, out_shape=jax.ShapeDtypeStruct((ASSETS, COLS)...  2.95 us

profile of v5, /device:TPU:120, one launch (start us, length us, event | category | flops | bytes accessed | tf_op | source)
XLA Modules:
  0.0 28.7 jit_solution(6522068673793995971)
XLA Ops:
  0.7 25.1 %shard_map.46 = (f32[4,2,2,4,2,8,512]{6,5,4,3,2,1,0:T(8,128)S(1)}, bf16[5,256,512]{2,1,0:T(8,128)(2,1)S(1)}, f32[1536,512]{1,0:T(8,128)S(1)}, s32[1,2048]{1,0:T(1,128)S(1)}, s32[1,2048]{1,0:T(1,128)S(1)}) custom-call(f32[16,512]{1,0:T(8,128)} %returns_ref.1, s32[1]{0:T(128)S(6)} %copy.5.windows_ref, s32[1,2048]{1,0:T(1,128)} %bitcast.3, s32[1,2048]{1,0:T(1,128)} %bitcast.4), custom_call_target="tpu_custom_call" | custom-call | tf_op jit(solution)/shard_map/pallas_call | solution.py:380
  25.8 2.9 %shard_map.47 = f32[2048,512]{1,0:T(8,128)} custom-call(s32[1]{0:T(128)S(6)} %copy.5.windows_ref, f32[4,2,2,4,2,8,512]{6,5,4,3,2,1,0:T(8,128)S(1)} %get-tuple-element.10.all_ref, bf16[5,256,512]{2,1,0:T(8,128)(2,1)S(1)} %get-tuple-element.11.own_ref, f32[1536,512]{1,0:T(8,128)S(1)} %get-tuple-element.12.done_ref, s32[1,2048]{1,0:T(1,128)S(1)} %get-tuple-element.13.from_ref, ...), custom_call_target="tpu_custom_call" | custom-call | tf_op jit(solution)/shard_map/pallas_call | solution.py:435

commit v6 on v5

--- a/solution.py
+++ b/solution.py
@@ -347,7 +347,7 @@
     return first, last
 
 
-def correlate(wide, rows, own_ref, own_spans, out_ref):
+def correlate(wide, rows, own_ref, own_spans, out_ref, after=None):
     first, last = rows
     live, high, low, sq_high, sq_low = (wide[i] for i in range(5))
     for n in range(0, COLS, TILE):
@@ -370,6 +370,8 @@
         var_l = jnp.maximum(pairs * square_l - sum_l * sum_l, pairs)
         var_r = jnp.maximum(pairs * square_r - sum_r * sum_r, pairs)
         out_ref[:, at] = covariance * lax.rsqrt(var_l * var_r)
+        if after is not None:
+            after(n)
 
 
 def gathered(returns, windows, listed_from, listed_until):
@@ -424,8 +426,16 @@
         now = rows
         if i < 7:
             rows = ready(i + 1)
-        correlate(wides[i % 2], now, own_ref, own_spans, result.at[i - FIRST])
-        store(result.at[i - FIRST], i)
+
+        def tile_done(n, i=i):
+            rows_of, cols = pl.ds(place_of(i, y)[1], ROWS), pl.ds(n, TILE)
+            src = result.at[i - FIRST, :, cols]
+            copies.append(pltpu.make_async_copy(src, out_ref.at[rows_of, cols], sems.at[i + n // TILE]))
+            copies[-1].start()
+
+        correlate(wides[i % 2], now, own_ref, own_spans, result.at[i - FIRST], tile_done if i == 7 else None)
+        if i < 7:
+            store(result.at[i - FIRST], i)
     for copy in copies:
         copy.wait()
 
@@ -438,7 +448,7 @@
         in_specs=[smem, vmem, vmem, vmem, vmem, vmem],
         out_specs=pl.BlockSpec(memory_space=pltpu.HBM),
         scratch_shapes=[pltpu.VMEM((5, ROWS, SPAN), BF16)] * 2
-        + [pltpu.VMEM((8 - FIRST, ROWS, COLS), F32), pltpu.SemaphoreType.DMA((8,))],
+        + [pltpu.VMEM((8 - FIRST, ROWS, COLS), F32), pltpu.SemaphoreType.DMA((9,))],
         compiler_params=pltpu.CompilerParams(vmem_limit_bytes=20 << 20),
     )(windows, whole, own, done, listed_from, listed_until)
 

time: 28.8 us -> 28.7 us (level)
  no operation moved by 1% of the time
where the time goes in v6:
time: 28.7 us; the launch traced here: 28.6 us
  Pallas kernels  28 us (98%)
  between operations  0.66 us (2%)
    pallas_call x1, Pallas kernels, gathered(): pl.pallas_call(gather_kernel, out_shape=[jax.ShapeDtypeStruct((NY, 2, 2,...  25.1 us
    pallas_call x1, Pallas kernels, completed(): pl.pallas_call(rest_kernel, out_shape=jax.ShapeDtypeStruct((ASSETS, COLS)...  2.87 us

profile of v6, /device:TPU:120, one launch (start us, length us, event | category | flops | bytes accessed | tf_op | source)
XLA Modules:
  0.0 28.6 jit_solution(10534818832980524493)
XLA Ops:
  0.7 25.1 %shard_map.46 = (f32[4,2,2,4,2,8,512]{6,5,4,3,2,1,0:T(8,128)S(1)}, bf16[5,256,512]{2,1,0:T(8,128)(2,1)S(1)}, f32[1536,512]{1,0:T(8,128)S(1)}, s32[1,2048]{1,0:T(1,128)S(1)}, s32[1,2048]{1,0:T(1,128)S(1)}) custom-call(f32[16,512]{1,0:T(8,128)} %returns_ref.1, s32[1]{0:T(128)S(6)} %copy.5.windows_ref, s32[1,2048]{1,0:T(1,128)} %bitcast.3, s32[1,2048]{1,0:T(1,128)} %bitcast.4), custom_call_target="tpu_custom_call" | custom-call | tf_op jit(solution)/shard_map/pallas_call | solution.py:382
  25.8 2.9 %shard_map.47 = f32[2048,512]{1,0:T(8,128)} custom-call(s32[1]{0:T(128)S(6)} %copy.5.windows_ref, f32[4,2,2,4,2,8,512]{6,5,4,3,2,1,0:T(8,128)S(1)} %get-tuple-element.10.all_ref, bf16[5,256,512]{2,1,0:T(8,128)(2,1)S(1)} %get-tuple-element.11.own_ref, f32[1536,512]{1,0:T(8,128)S(1)} %get-tuple-element.12.done_ref, s32[1,2048]{1,0:T(1,128)S(1)} %get-tuple-element.13.from_ref, ...), custom_call_target="tpu_custom_call" | custom-call | tf_op jit(solution)/shard_map/pallas_call | solution.py:445
